TPU v7x, 256 devices: a whole 4x4x8 slice. The times are simulated.
256 devices in a mesh: pool: 16 (over y, x), slab: 16 (over z, core).
Axes of the slice: x: 4, y: 4, z: 8, core: 2. Of those that a mesh axis runs over, the one named last changes fastest.
Arguments:
- wave_coeff: bfloat16 [256, 2, 96, 9216], P(('pool', 'slab')), may hold values from -6 to 6
- response_coeff: bfloat16 [256, 2, 96, 9216], P(('pool', 'slab')), may hold values from -6 to 6
- band_index: int32 [256], P(('pool', 'slab')), may hold values from 0 to 255, each once
- occupation: int32 [256], replicated, may hold values from 0 to 2
- local_kernel: float32 [96, 9216], P('slab'), may hold values from 0.5 to 4
- gradient_kernel: float32 [96, 9216], P('slab'), may hold values from 0.25 to 2.5
Outputs:
- induced_potential: float32 [96, 9216], P('slab', 'pool')
Inputs may be any that keep to these rules, and one draw needn't show every extreme that they name: `band_index`: a permutation of the 256 band numbers.
All inputs are finite; a program needn't handle non-finite values.
Results may differ from a plain program's by a relative error of at most 0.0067.
Values sent between devices are 32-bit elements; how exact they have to be, the bound alone decides.
A program may use at most 128 MiB of HBM per device.

v0:
```python
import math

import jax
import jax.numpy as jnp
from jax import lax
from jax.sharding import PartitionSpec as P

full_turn = 2.0 * math.pi


def split_up(array, dim, length):
    before, after = (array.shape[:dim], array.shape[dim + 1 :])
    return jnp.moveaxis(array.reshape(*before, length, -1, *after), dim, 0)


def sent_and_summed(array, axis, dim):
    length = lax.axis_size(axis)
    parts = lax.all_to_all(split_up(array, dim, length), axis, 0, 0, tiled=True)
    return jnp.sum(parts, axis=0)


def padded_2(array, sides, width):
    edges = {}
    for axis, dim in sides:
        size, length = (lax.axis_size(axis), array.shape[dim])
        up = [(i, (i + 1) % size) for i in range(size)]
        last = lax.slice_in_dim(array, length - width, length, axis=dim)
        leading = lax.slice_in_dim(array, 0, width, axis=dim)
        edges[dim] = (
            lax.ppermute(last, axis, up),
            lax.ppermute(leading, axis, [(b, a) for a, b in up]),
        )
    done = []
    for _, dim in sides:
        low, high = edges[dim]
        around = [(width, width) if d in done else (0, 0) for d in range(array.ndim)]
        array = jnp.concatenate([jnp.pad(low, around), array, jnp.pad(high, around)], axis=dim)
        done.append(dim)
    return array


def stacked_table(length, sign, dtype):
    indices = jnp.arange(length, dtype=jnp.int32)
    product = indices[:, None] * indices[None, :] % length
    angles = product.astype(jnp.float32) * (full_turn / length)
    factor = 1.0 / math.sqrt(length)
    cosine = jnp.cos(angles) * factor
    sine_part = jnp.sin(angles) * factor
    upper_half = jnp.stack([cosine, -sign * sine_part], axis=1)
    lower_half = jnp.stack([sign * sine_part, cosine], axis=1)
    return jnp.stack([upper_half, lower_half], axis=0).astype(dtype)


def signed_freq(length, first_wave, amount):
    waves = first_wave + jnp.arange(amount, dtype=jnp.int32)
    return jnp.where(2 * waves >= length, waves - length, waves).astype(jnp.float32)


def coulomb_kernel(length, starts, counts):
    first_freq = signed_freq(length, starts[0], counts[0])[:, None, None]
    second_freq = signed_freq(length, starts[1], counts[1])[None, :, None]
    third_freq = signed_freq(length, starts[2], counts[2])[None, None, :]
    squared = (full_turn / length) ** 2 * (
        first_freq * first_freq + second_freq * second_freq + third_freq * third_freq
    )
    nonzero = jnp.where(squared > 0, squared, 1.0)
    return jnp.where(squared > 0, full_turn / nonzero, 0.0)


def exact_pass(spec, tables, values):
    return jnp.einsum(
        spec, tables, values, precision=lax.Precision.HIGHEST, preferred_element_type=jnp.float32
    )


def half_pass(spec, tables, values):
    return jnp.einsum(spec, tables, values, preferred_element_type=jnp.float32)


def band_weights(band_index, occupation):
    numbers = jnp.arange(occupation.shape[0], dtype=jnp.int32)
    matches = band_index[:, None] == numbers[None, :]
    return jnp.sum(jnp.where(matches, occupation[None, :], 0), axis=1).astype(jnp.float32)


def weighted_intersection(wave_space, response_space, weights, factor):
    intersection = wave_space[:, 0] * response_space[:, 0] + wave_space[:, 1] * response_space[:, 1]
    return jnp.sum(weights[:, None, None, None] * intersection, axis=0) * factor


def flux_divergence(padded, coefficient):
    interior = padded[2:-2, 2:-2]
    depth_flux = coefficient[1:-1, 2:-2] * ((padded[2:, 2:-2] - padded[:-2, 2:-2]) * 0.5)
    depth_div = (depth_flux[2:] - depth_flux[:-2]) * 0.5
    across_flux = coefficient[2:-2, 1:-1] * ((padded[2:-2, 2:] - padded[2:-2, :-2]) * 0.5)
    across_div = (across_flux[:, 2:] - across_flux[:, :-2]) * 0.5
    along_flux = coefficient[2:-2, 2:-2] * (
        (jnp.roll(interior, -1, 2) - jnp.roll(interior, 1, 2)) * 0.5
    )
    along_div = (jnp.roll(along_flux, -1, 2) - jnp.roll(along_flux, 1, 2)) * 0.5
    return (interior, depth_div + across_div + along_div)


def shards(wave_coeff, response_coeff, band_index, occupation, local_kernel, gradient_kernel):
    length = wave_coeff.shape[2]
    band_count = wave_coeff.shape[0]
    slab_count = lax.axis_size("slab")
    pool_count = lax.axis_size("pool")
    planes = length // slab_count
    columns = length // pool_count
    slab_width = length // slab_count
    slab_rank = lax.axis_index("slab")
    pool_rank = lax.axis_index("pool")
    first_row = pool_rank * columns
    factor = 1.0 / occupation.shape[0]
    inverse_half = stacked_table(length, 1.0, jnp.bfloat16)
    forward_full = stacked_table(length, -1.0, jnp.float32)
    inverse_full = stacked_table(length, 1.0, jnp.float32)
    weights = band_weights(band_index, occupation)
    cube_shape = (band_count, 2, length, length, length)
    wave_planes = half_pass(
        "rzsk,bskxy->brzxy", inverse_half, wave_coeff.reshape(cube_shape)
    ).astype(jnp.bfloat16)
    response_planes = half_pass(
        "rzsk,bskxy->brzxy", inverse_half, response_coeff.reshape(cube_shape)
    ).astype(jnp.bfloat16)
    wave_rows = half_pass("rxsk,bszky->brzxy", inverse_half, wave_planes).astype(jnp.bfloat16)
    response_rows = half_pass("rxsk,bszky->brzxy", inverse_half, response_planes).astype(
        jnp.bfloat16
    )
    wave_space = half_pass("rysk,bszxk->brzxy", inverse_half, wave_rows)
    response_space = half_pass("rysk,bszxk->brzxy", inverse_half, response_rows)
    slab_part = lax.psum_scatter(
        weighted_intersection(wave_space, response_space, weights, factor).reshape(
            planes * lax.axis_size("slab"), length * length
        ),
        "slab",
        scatter_dimension=0,
        tiled=True,
    )
    density_block = sent_and_summed(slab_part, "pool", 1).reshape(planes, columns, length)
    complex_block = jnp.stack([density_block, jnp.zeros_like(density_block)])
    along_done = exact_pass("rysk,szxk->rzxy", forward_full, complex_block)
    first_turned = lax.all_to_all(along_done, "pool", split_axis=3, concat_axis=2, tiled=True)
    across_done = exact_pass("rxsk,szky->rzxy", forward_full, first_turned)
    second_turned = lax.all_to_all(across_done, "slab", split_axis=2, concat_axis=1, tiled=True)
    kernel = coulomb_kernel(
        length, (0, slab_rank * slab_width, pool_rank * columns), (length, slab_width, columns)
    )
    scaled = exact_pass("rzsk,skxy->rzxy", forward_full, second_turned) * kernel[None]
    second_back = lax.all_to_all(
        exact_pass("rzsk,skxy->rzxy", inverse_full, scaled),
        "slab",
        split_axis=1,
        concat_axis=2,
        tiled=True,
    )
    first_back = lax.all_to_all(
        exact_pass("rxsk,szky->rzxy", inverse_full, second_back),
        "pool",
        split_axis=2,
        concat_axis=3,
        tiled=True,
    )
    hartree = exact_pass("rysk,szxk->rzxy", inverse_full[0:1], first_back)[0]
    gradient_block = lax.dynamic_slice_in_dim(
        gradient_kernel.reshape(planes, length, length), first_row, columns, 1
    )
    padded_density, padded_coefficient = (
        padded_2(density_block, (("pool", 1), ("slab", 0)), 2),
        padded_2(gradient_block, (("pool", 1), ("slab", 0)), 2),
    )
    local_block = lax.dynamic_slice_in_dim(
        local_kernel.reshape(planes, length, length), first_row, columns, 1
    )
    interior, divergence = flux_divergence(padded_density, padded_coefficient)
    potential = hartree + local_block * interior - divergence
    return potential.reshape(planes, columns * length)


def solution(mesh):
    return jax.shard_map(
        shards,
        mesh=mesh,
        in_specs=(
            P(("pool", "slab"), None, None, None),
            P(("pool", "slab"), None, None, None),
            P(("pool", "slab")),
            P(),
            P("slab", None),
            P("slab", None),
        ),
        out_specs=P("slab", "pool"),
        check_vma=False,
    )
```

profile of v0, /device:TPU:1, one launch (start us, length us, event | category | flops | bytes accessed | tf_op | source)
XLA Modules:
  0.0 241.1 jit_solution(8773639654375715844)
XLA Ops:
  0.5 7.8 %reshape.230 = bf16[2,96,96,96]{3,2,1,0:T(8,128)(2,1)} reshape(bf16[1,2,96,9216]{3,2,1,0:T(8,128)(2,1)} %param.7) | data formatting | bytes 7077888 | tf_op jit(solution)/shard_map/reshape.16
  9.7 6.9 %fusion.5 = bf16[2,96,96,96,1]{3,1,2,0,4:T(8,128)(2,1)} fusion(bf16[2,96,96,96]{3,2,1,0:T(8,128)(2,1)} %reshape.230, bf16[2,96,2,96]{3,1,2,0:T(8,128)(2,1)S(1)} %fusion.46), kind=kOutput, calls=%fused_computation.7 | convolution fusion | flops 681246720 | bytes 7151616 | tf_op jit(solution)/shard_map/rzsk,bskxy->brzxy/dot_general | solution.py:77
  16.6 8.9 %fusion.22 = f32[1,2,96,96,96]{4,3,1,2,0:T(8,128)} fusion(bf16[2,96,96,96,1]{3,1,2,0,4:T(8,128)(2,1)} %fusion.5, bf16[2,96,2,96]{3,1,2,0:T(8,128)(2,1)S(1)} %fusion.46), kind=kOutput, calls=%fused_computation.25 | convolution fusion | flops 1360723968 | bytes 10690560 | tf_op jit(solution)/shard_map/rysk,bszxk->brzxy/dot_general | solution.py:77
  25.5 7.8 %reshape.228 = bf16[2,96,96,96]{3,2,1,0:T(8,128)(2,1)} reshape(bf16[1,2,96,9216]{3,2,1,0:T(8,128)(2,1)} %param.6) | data formatting | bytes 7077888 | tf_op jit(solution)/shard_map/reshape.2
  33.3 6.9 %fusion.1 = bf16[2,96,96,96,1]{3,1,2,0,4:T(8,128)(2,1)} fusion(bf16[2,96,96,96]{3,2,1,0:T(8,128)(2,1)} %reshape.228, bf16[2,96,2,96]{3,1,2,0:T(8,128)(2,1)S(1)} %fusion.46), kind=kOutput, calls=%fused_computation.4 | convolution fusion | flops 681246720 | bytes 7151616 | tf_op jit(solution)/shard_map/rzsk,bskxy->brzxy/dot_general | solution.py:77
  40.2 8.8 %fusion.25 = f32[1,2,96,96,96]{4,3,1,2,0:T(8,128)} fusion(bf16[2,96,96,96,1]{3,1,2,0,4:T(8,128)(2,1)} %fusion.1, bf16[2,96,2,96]{3,1,2,0:T(8,128)(2,1)S(1)} %fusion.46), kind=kOutput, calls=%fused_computation.26 | convolution fusion | flops 1360723968 | bytes 10690560 | tf_op jit(solution)/shard_map/rysk,bszxk->brzxy/dot_general | solution.py:77
  51.0 9.8 %fusion.11 = f32[1,1,96,96,96]{4,3,1,2,0:T(8,128)} fusion(f32[1,2,96,96,96]{4,3,1,2,0:T(8,128)} %fusion.22, f32[1,2,96,96,96]{4,3,1,2,0:T(8,128)} %fusion.25, f32[]{:T(128)S(6)} %convert_element_type.98), kind=kLoop, calls=%fused_computation.13 | loop fusion | flops 4423680 | bytes 17694724 | tf_op jit(solution)/shard_map/mul | solution.py:88
  60.9 4.6 %mul.324 = f32[96,9216]{1,0:T(8,128)S(1)} reshape(f32[1,1,96,96,96]{4,3,1,2,0:T(8,128)} %fusion.11) | data formatting | bytes 7077888 | tf_op jit(solution)/shard_map/mul | solution.py:88
  65.5 40.3 %fusion = f32[8,9216]{1,0:T(8,128)} fusion(f32[96,9216]{1,0:T(8,128)S(1)} %mul.324), kind=kCustom, calls=%all-reduce-scatter | all-reduce-scatter fusion | flops 1179649 | bytes 3834880
  107.3 4.0 %collective-permute-start.9 = (f32[8,9216]{1,0:T(8,128)}, f32[8,9216]{1,0:T(8,128)S(1)}, u32[]{:S(2)}, u32[]{:S(2)}) collective-permute-start(f32[8,9216]{1,0:T(8,128)} %fusion), channel_id=1, source_target_pairs={{0,2},{1,3},{2,4},{3,5},{4,6},{5,7},{6,8},{7,9},{8,10},{9,11},{10,... | collective-permute-start | bytes 884744
  111.3 4.3 %collective-permute-start.8 = (f32[8,9216]{1,0:T(8,128)}, f32[8,9216]{1,0:T(8,128)S(1)}, u32[]{:S(2)}, u32[]{:S(2)}) collective-permute-start(f32[8,9216]{1,0:T(8,128)} %fusion), channel_id=1, source_target_pairs={{0,1},{1,2},{2,3},{3,4},{4,5},{5,6},{6,7},{7,8},{8,9},{9,10},{10,1... | collective-permute-start | bytes 884744
  116.6 5.1 %collective-permute-start.11 = (f32[6,9216]{1,0:T(8,128)S(1)}, f32[6,9216]{1,0:T(8,128)S(1)}, u32[]{:S(2)}, u32[]{:S(2)}) collective-permute-start(f32[6,9216]{1,0:T(8,128)S(1)} %slice.150), channel_id=1, source_target_pairs={{0,4},{1,5},{2,6},{3,7},{4,8},{5,9},{6,10},{7,11},{8,12},{9,13},{1... | collective-permute-start | bytes 663560
  122.8 5.0 %collective-permute-start.2 = (f32[6,2,96]{2,1,0:T(2,128)S(1)}, f32[6,2,96]{2,1,0:T(2,128)S(1)}, u32[]{:S(2)}, u32[]{:S(2)}) collective-permute-start(f32[6,2,96]{2,1,0:T(2,128)S(1)} %get-tuple-element.10), channel_id=1, source_target_pairs={{16,0},{32,16},{48,32},{64,48},{80,64},{96,80},{112,96},{128,112},... | collective-permute-start | bytes 13832 | tf_op jit(solution)/shard_map/ppermute | solution.py:31
  132.9 6.5 %collective-permute-start = (f32[2,6,96]{2,1,0:T(8,128)S(1)}, f32[2,6,96]{2,1,0:T(8,128)S(1)}, u32[]{:S(2)}, u32[]{:S(2)}) collective-permute-start(f32[2,6,96]{2,1,0:T(8,128)S(1)} %get-tuple-element.7), channel_id=1, source_target_pairs={{0,1},{1,2},{2,3},{3,4},{4,5},{5,6},{6,7},{7,8},{8,9},{9,10},{10,1... | collective-permute-start | bytes 13832 | tf_op jit(solution)/shard_map/ppermute | solution.py:30
  139.3 4.3 %concatenate.47 = f32[38,9216]{1,0:T(8,128)S(1)} concatenate(f32[6,9216]{1,0:T(8,128)S(1)} %collective-permute-done.11, f32[8,9216]{1,0:T(8,128)S(1)} %collective-permute-done.10, f32[8,9216]{1,0:T(8,128)S(1)} %collective-permute-done.9, f32[8,9216]{1,0:T(8,128)S(1)} %collective-permute-done.8, f32[8,9216]{1,0:T(8,128)} %fusion), dimensions={0} | concatenate | bytes 2801664
  144.6 6.5 %all-to-all-start = ((f32[16,6,576]{2,1,0:T(8,128)}), f32[16,6,576]{2,1,0:T(8,128)S(1)}, u32[]{:S(2)}, u32[]{:S(2)}) async-start(f32[16,6,576]{2,1,0:T(8,128)} %bitcast.212), calls=%async_computation | async-start | bytes 655360 | tf_op jit(solution)/shard_map/all_to_all | solution.py:18
  151.1 7.8 %all-to-all-done = f32[16,6,576]{2,1,0:T(8,128)S(1)} async-done(((f32[16,6,576]{2,1,0:T(8,128)}), f32[16,6,576]{2,1,0:T(8,128)S(1)}, u32[]{:S(2)}, u32[]{:S(2)}) %all-to-all-start) | async-done | bytes 221216 | tf_op jit(solution)/shard_map/all_to_all | solution.py:18
  160.3 1.6 reshape.265
  161.8 3.5 %all-to-all-start.1 = ((f32[16,1,432]{2,1,0:T(1,128)}), f32[16,1,432]{2,1,0:T(1,128)S(1)}, u32[]{:S(2)}, u32[]{:S(2)}) async-start(f32[16,1,432]{2,1,0:T(1,128)} %reshape.265), calls=%async_computation.1 | async-start | bytes 65536 | tf_op jit(solution)/shard_map/all_to_all | solution.py:144
  165.3 6.4 %all-to-all-done.1 = f32[16,1,432]{2,1,0:T(1,128)S(1)} async-done(((f32[16,1,432]{2,1,0:T(1,128)}), f32[16,1,432]{2,1,0:T(1,128)S(1)}, u32[]{:S(2)}, u32[]{:S(2)}) %all-to-all-start.1) | async-done | bytes 27680 | tf_op jit(solution)/shard_map/all_to_all | solution.py:144
  174.9 1.6 reshape.267
  176.4 15.4 %all-to-all-start.2 = ((f32[16,1,432]{2,1,0:T(1,128)}), f32[16,1,432]{2,1,0:T(1,128)S(1)}, u32[]{:S(2)}, u32[]{:S(2)}) async-start(f32[16,1,432]{2,1,0:T(1,128)} %reshape.267), calls=%async_computation.2 | async-start | bytes 65536 | tf_op jit(solution)/shard_map/all_to_all | solution.py:146
  191.8 1.6 collective-permute-start.5
  193.5 5.7 %all-to-all-done.2 = f32[16,1,432]{2,1,0:T(1,128)S(1)} async-done(((f32[16,1,432]{2,1,0:T(1,128)}), f32[16,1,432]{2,1,0:T(1,128)S(1)}, u32[]{:S(2)}, u32[]{:S(2)}) %all-to-all-start.2) | async-done | bytes 27680 | tf_op jit(solution)/shard_map/all_to_all | solution.py:146
  200.7 1.6 copy.109
  205.1 1.6 reshape.269
  206.7 6.1 %all-to-all-start.3 = ((f32[16,1,432]{2,1,0:T(1,128)}), f32[16,1,432]{2,1,0:T(1,128)S(1)}, u32[]{:S(2)}, u32[]{:S(2)}) async-start(f32[16,1,432]{2,1,0:T(1,128)} %reshape.269), calls=%async_computation.3 | async-start | bytes 65536 | tf_op jit(solution)/shard_map/all_to_all | solution.py:151
  212.8 7.4 %all-to-all-done.3 = f32[16,1,432]{2,1,0:T(1,128)S(1)} async-done(((f32[16,1,432]{2,1,0:T(1,128)}), f32[16,1,432]{2,1,0:T(1,128)S(1)}, u32[]{:S(2)}, u32[]{:S(2)}) %all-to-all-start.3) | async-done | bytes 27680 | tf_op jit(solution)/shard_map/all_to_all | solution.py:151
  221.7 1.6 copy.113
  224.4 1.6 reshape.271
  225.9 5.9 %all-to-all-start.4 = ((f32[16,1,432]{2,1,0:T(1,128)}), f32[16,1,432]{2,1,0:T(1,128)S(1)}, u32[]{:S(2)}, u32[]{:S(2)}) async-start(f32[16,1,432]{2,1,0:T(1,128)} %reshape.271), calls=%async_computation.4 | async-start | bytes 65536 | tf_op jit(solution)/shard_map/all_to_all | solution.py:158
  231.9 6.4 %all-to-all-done.4 = f32[16,1,432]{2,1,0:T(1,128)S(1)} async-done(((f32[16,1,432]{2,1,0:T(1,128)}), f32[16,1,432]{2,1,0:T(1,128)S(1)}, u32[]{:S(2)}, u32[]{:S(2)}) %all-to-all-start.4) | async-done | bytes 27680 | tf_op jit(solution)/shard_map/all_to_all | solution.py:158
  (101 shorter events, 25.7 us)
Async XLA Ops:
  0.2 8.8 %copy-start.6 = (f32[96,1,96]{2,0,1:T(8,128)}, f32[96,1,96]{2,0,1:T(8,128)S(1)}, u32[]{:S(2)}) copy-start(f32[96,1,96]{2,0,1:T(8,128)S(1)} %get-tuple-element.29) | copy-start | bytes 110596
  0.2 8.8 %copy-start.8 = (f32[96,1,96]{2,0,1:T(8,128)}, f32[96,1,96]{2,0,1:T(8,128)S(1)}, u32[]{:S(2)}) copy-start(f32[96,1,96]{2,0,1:T(8,128)S(1)} %get-tuple-element.30) | copy-start | bytes 110596
  9.0 0.6 copy-start.2
  9.0 0.7 copy-start.4
  40.2 9.5 %copy-start.10 = (s32[256]{0:T(256)S(1)}, s32[256]{0:T(256)}, u32[]{:S(2)}) copy-start(s32[256]{0:T(256)} %param.9) | copy-start | bytes 3076
  65.5 63.4 %copy-start.11 = (u32[256]{0:T(256)S(1)}, u32[256]{0:T(256)}, u32[]{:S(2)}) copy-start(u32[256]{0:T(256)} %constant.78) | copy-start | bytes 3076
  105.8 53.7 %copy-start = (f32[1,96,2,96]{3,1,2,0:T(8,128)S(1)}, f32[1,96,2,96]{3,1,2,0:T(8,128)}, u32[]{:S(2)}) copy-start(f32[1,96,2,96]{3,1,2,0:T(8,128)} %get-tuple-element.11) | copy-start | bytes 221188
  105.8 53.7 %copy-start.1 = (f32[1,96,2,96]{3,1,2,0:T(8,128)S(1)}, f32[1,96,2,96]{3,1,2,0:T(8,128)}, u32[]{:S(2)}) copy-start(f32[1,96,2,96]{3,1,2,0:T(8,128)} %get-tuple-element.16) | copy-start | bytes 221188
  105.8 25.9 %collective-permute-start.10 = (f32[8,9216]{1,0:T(8,128)}, f32[8,9216]{1,0:T(8,128)S(1)}, u32[]{:S(2)}, u32[]{:S(2)}) collective-permute-start(f32[8,9216]{1,0:T(8,128)} %fusion), channel_id=1, source_target_pairs={{0,3},{1,4},{2,5},{3,6},{4,7},{5,8},{6,9},{7,10},{8,11},{9,12},{10... | collective-permute-start | bytes 884744
  107.3 25.6 %collective-permute-start.9 = (f32[8,9216]{1,0:T(8,128)}, f32[8,9216]{1,0:T(8,128)S(1)}, u32[]{:S(2)}, u32[]{:S(2)}) collective-permute-start(f32[8,9216]{1,0:T(8,128)} %fusion), channel_id=1, source_target_pairs={{0,2},{1,3},{2,4},{3,5},{4,6},{5,7},{6,8},{7,9},{8,10},{9,11},{10,... | collective-permute-start | bytes 884744
  111.3 28.0 %collective-permute-start.8 = (f32[8,9216]{1,0:T(8,128)}, f32[8,9216]{1,0:T(8,128)S(1)}, u32[]{:S(2)}, u32[]{:S(2)}) collective-permute-start(f32[8,9216]{1,0:T(8,128)} %fusion), channel_id=1, source_target_pairs={{0,1},{1,2},{2,3},{3,4},{4,5},{5,6},{6,7},{7,8},{8,9},{9,10},{10,1... | collective-permute-start | bytes 884744
  116.6 13.9 %collective-permute-start.11 = (f32[6,9216]{1,0:T(8,128)S(1)}, f32[6,9216]{1,0:T(8,128)S(1)}, u32[]{:S(2)}, u32[]{:S(2)}) collective-permute-start(f32[6,9216]{1,0:T(8,128)S(1)} %slice.150), channel_id=1, source_target_pairs={{0,4},{1,5},{2,6},{3,7},{4,8},{5,9},{6,10},{7,11},{8,12},{9,13},{1... | collective-permute-start | bytes 663560
  122.8 80.2 %collective-permute-start.2 = (f32[6,2,96]{2,1,0:T(2,128)S(1)}, f32[6,2,96]{2,1,0:T(2,128)S(1)}, u32[]{:S(2)}, u32[]{:S(2)}) collective-permute-start(f32[6,2,96]{2,1,0:T(2,128)S(1)} %get-tuple-element.10), channel_id=1, source_target_pairs={{16,0},{32,16},{48,32},{64,48},{80,64},{96,80},{112,96},{128,112},... | collective-permute-start | bytes 13832 | tf_op jit(solution)/shard_map/ppermute | solution.py:31
  130.5 73.1 %collective-permute-start.1 = (f32[6,2,96]{2,1,0:T(2,128)S(1)}, f32[6,2,96]{2,1,0:T(2,128)S(1)}, u32[]{:S(2)}, u32[]{:S(2)}) collective-permute-start(f32[6,2,96]{2,1,0:T(2,128)S(1)} %get-tuple-element.9), channel_id=1, source_target_pairs={{0,16},{16,32},{32,48},{48,64},{64,80},{80,96},{96,112},{112,128},... | collective-permute-start | bytes 13832 | tf_op jit(solution)/shard_map/ppermute | solution.py:30
  131.7 72.7 %collective-permute-start.3 = (f32[2,6,96]{2,1,0:T(8,128)S(1)}, f32[2,6,96]{2,1,0:T(8,128)S(1)}, u32[]{:S(2)}, u32[]{:S(2)}) collective-permute-start(f32[2,6,96]{2,1,0:T(8,128)S(1)} %get-tuple-element.8), channel_id=1, source_target_pairs={{1,0},{2,1},{3,2},{4,3},{5,4},{6,5},{7,6},{8,7},{9,8},{10,9},{11,1... | collective-permute-start | bytes 13832 | tf_op jit(solution)/shard_map/ppermute | solution.py:31
  132.9 79.9 %collective-permute-start = (f32[2,6,96]{2,1,0:T(8,128)S(1)}, f32[2,6,96]{2,1,0:T(8,128)S(1)}, u32[]{:S(2)}, u32[]{:S(2)}) collective-permute-start(f32[2,6,96]{2,1,0:T(8,128)S(1)} %get-tuple-element.7), channel_id=1, source_target_pairs={{0,1},{1,2},{2,3},{3,4},{4,5},{5,6},{6,7},{7,8},{8,9},{9,10},{10,1... | collective-permute-start | bytes 13832 | tf_op jit(solution)/shard_map/ppermute | solution.py:30
  144.6 14.4 %all-to-all-start = ((f32[16,6,576]{2,1,0:T(8,128)}), f32[16,6,576]{2,1,0:T(8,128)S(1)}, u32[]{:S(2)}, u32[]{:S(2)}) async-start(f32[16,6,576]{2,1,0:T(8,128)} %bitcast.212), calls=%async_computation | async-start | bytes 655360 | tf_op jit(solution)/shard_map/all_to_all | solution.py:18
  159.0 45.4 %copy-start.3 = (f32[1,96,2,96]{3,1,2,0:T(8,128)S(1)}, f32[1,96,2,96]{3,1,2,0:T(8,128)}, u32[]{:S(2)}) copy-start(f32[1,96,2,96]{3,1,2,0:T(8,128)} %copy-done.2) | copy-start | bytes 221188
  159.0 45.4 %copy-start.5 = (f32[1,96,2,96]{3,1,2,0:T(8,128)S(1)}, f32[1,96,2,96]{3,1,2,0:T(8,128)}, u32[]{:S(2)}) copy-start(f32[1,96,2,96]{3,1,2,0:T(8,128)} %copy-done.4) | copy-start | bytes 221188
  161.8 9.9 %all-to-all-start.1 = ((f32[16,1,432]{2,1,0:T(1,128)}), f32[16,1,432]{2,1,0:T(1,128)S(1)}, u32[]{:S(2)}, u32[]{:S(2)}) async-start(f32[16,1,432]{2,1,0:T(1,128)} %reshape.265), calls=%async_computation.1 | async-start | bytes 65536 | tf_op jit(solution)/shard_map/all_to_all | solution.py:144
  176.4 22.8 %all-to-all-start.2 = ((f32[16,1,432]{2,1,0:T(1,128)}), f32[16,1,432]{2,1,0:T(1,128)S(1)}, u32[]{:S(2)}, u32[]{:S(2)}) async-start(f32[16,1,432]{2,1,0:T(1,128)} %reshape.267), calls=%async_computation.2 | async-start | bytes 65536 | tf_op jit(solution)/shard_map/all_to_all | solution.py:146
  191.8 20.9 %collective-permute-start.5 = (f32[6,2,96]{2,1,0:T(2,128)S(1)}, f32[6,2,96]{2,1,0:T(2,128)S(1)}, u32[]{:S(2)}, u32[]{:S(2)}) collective-permute-start(f32[6,2,96]{2,1,0:T(2,128)S(1)} %get-tuple-element.22), channel_id=1, source_target_pairs={{16,0},{32,16},{48,32},{64,48},{80,64},{96,80},{112,96},{128,112},... | collective-permute-start | bytes 13832 | tf_op jit(solution)/shard_map/ppermute | solution.py:31
  202.3 37.9 %copy-start.7 = (f32[96,1,96]{2,0,1:T(8,128)S(1)}, f32[96,1,96]{2,0,1:T(8,128)}, u32[]{:S(2)}) copy-start(f32[96,1,96]{2,0,1:T(8,128)} %copy-done.6) | copy-start | bytes 110596
  202.3 37.9 %copy-start.9 = (f32[96,1,96]{2,0,1:T(8,128)S(1)}, f32[96,1,96]{2,0,1:T(8,128)}, u32[]{:S(2)}) copy-start(f32[96,1,96]{2,0,1:T(8,128)} %copy-done.8) | copy-start | bytes 110596
  203.0 9.8 %collective-permute-start.4 = (f32[6,2,96]{2,1,0:T(2,128)S(1)}, f32[6,2,96]{2,1,0:T(2,128)S(1)}, u32[]{:S(2)}, u32[]{:S(2)}) collective-permute-start(f32[6,2,96]{2,1,0:T(2,128)S(1)} %get-tuple-element.21), channel_id=1, source_target_pairs={{0,16},{16,32},{32,48},{48,64},{64,80},{80,96},{96,112},{112,128},... | collective-permute-start | bytes 13832 | tf_op jit(solution)/shard_map/ppermute | solution.py:30
  203.6 9.2 %collective-permute-start.7 = (f32[2,6,96]{2,1,0:T(8,128)S(1)}, f32[2,6,96]{2,1,0:T(8,128)S(1)}, u32[]{:S(2)}, u32[]{:S(2)}) collective-permute-start(f32[2,6,96]{2,1,0:T(8,128)S(1)} %slice.115), channel_id=1, source_target_pairs={{0,1},{1,2},{2,3},{3,4},{4,5},{5,6},{6,7},{7,8},{8,9},{9,10},{10,1... | collective-permute-start | bytes 13832 | tf_op jit(solution)/shard_map/ppermute | solution.py:30
  204.4 8.4 %collective-permute-start.6 = (f32[2,6,96]{2,1,0:T(8,128)S(1)}, f32[2,6,96]{2,1,0:T(8,128)S(1)}, u32[]{:S(2)}, u32[]{:S(2)}) collective-permute-start(f32[2,6,96]{2,1,0:T(8,128)S(1)} %slice.112), channel_id=1, source_target_pairs={{1,0},{2,1},{3,2},{4,3},{5,4},{6,5},{7,6},{8,7},{9,8},{10,9},{11,1... | collective-permute-start | bytes 13832 | tf_op jit(solution)/shard_map/ppermute | solution.py:31
  206.7 13.5 %all-to-all-start.3 = ((f32[16,1,432]{2,1,0:T(1,128)}), f32[16,1,432]{2,1,0:T(1,128)S(1)}, u32[]{:S(2)}, u32[]{:S(2)}) async-start(f32[16,1,432]{2,1,0:T(1,128)} %reshape.269), calls=%async_computation.3 | async-start | bytes 65536 | tf_op jit(solution)/shard_map/all_to_all | solution.py:151
  225.9 12.3 %all-to-all-start.4 = ((f32[16,1,432]{2,1,0:T(1,128)}), f32[16,1,432]{2,1,0:T(1,128)S(1)}, u32[]{:S(2)}, u32[]{:S(2)}) async-start(f32[16,1,432]{2,1,0:T(1,128)} %reshape.271), calls=%async_computation.4 | async-start | bytes 65536 | tf_op jit(solution)/shard_map/all_to_all | solution.py:158
where the time goes:
time: 242 us; the launch traced here: 241 us
  starting transfers between devices  68.9 us (28%)
  local copies, waits for them, and re-layouts  47.3 us (20%)
  blocking collectives  40.3 us (17%)
  waiting for transfers between devices  33.9 us (14%)
  matrix products  33.4 us (14%)
  other arithmetic  14.9 us (6%)
  between operations  2.44 us (1%)
    unnamed x1, blocking collectives  40.3 us
    dot_general x4, matrix products, half_pass(): return jnp.einsum(spec, tables, values, preferred_element_type=jnp.float32)  31.5 us
    unnamed x36, local copies, waits for them, and re-layouts  15.9 us
    another operation x2, local copies, waits for them, and re-layouts  15.7 us
    all_to_all x1, starting transfers between devices, shards(): lax.all_to_all(across_done, 'slab', split_axis=2, concat_axis=1, tiled=True)  15.4 us
    unnamed x4, starting transfers between devices  14.8 us
    mul x1, other arithmetic, weighted_intersection(): return jnp.sum(weights[:, None, None, None] * intersection, axis=0) * factor  9.85 us
    ppermute x4, starting transfers between devices, padded_2(): lax.ppermute(last, axis, up)  9.08 us
  transfers between devices with their start and end apart: 17, of which 6 were waited for; matrix products, arithmetic and copies ran while one was open for 9% of the time, Pallas kernels for 0%

commit v1 on v0

v1 whole, which is shorter than its diff:
```python
import math
import numpy as np
import jax, jax.numpy as jnp
from jax import lax
from jax.experimental import pallas as pl
from jax.experimental.pallas import tpu as pltpu
from jax.sharding import PartitionSpec as P

MESH = pl.DeviceIdType.MESH
full_turn = 2.0 * math.pi
N = 96

def np_tables():
    k = np.arange(N)
    ang = (np.outer(k, k) % N) * (2 * np.pi / N)
    c, s = np.cos(ang) / np.sqrt(N), np.sin(ang) / np.sqrt(N)
    t = np.block([[c, -s], [s, c]]).astype(np.float32)
    hu = (np.cos(ang) + np.sin(ang)).astype(np.float32)
    return t, hu

def y_tables(t):
    outs = []
    for row in range(4):
        js = sorted({(96 * row) // 128, (96 * row + 95) // 128})
        w = np.zeros((256 * len(js), 256), np.float32)
        for n, j in enumerate(js):
            for l in range(128):
                d = 128 * j + l
                if d // 96 != row:
                    continue
                ky = d % 96
                for s in range(2):
                    for r in range(2):
                        w[256 * n + 128 * s + l, 128 * r:128 * r + 96] = t[96 * r:96 * r + 96, 96 * s + ky]
        outs.append(w)
    return outs

def dense_tables(hu):
    outs = []
    for j in range(3):
        w = np.zeros((256, 128), np.float32)
        for l in range(128):
            d = 128 * j + l
            q, ky = d // 96, d % 96
            w[(q - j) * 128:(q - j) * 128 + 96, l] = hu[ky]
        outs.append(w)
    return np.stack(outs)

BL = 1536
NB = 9216 // BL

def kernel_a(occ, idx, wave, resp, t_ref, w0, w1, w2, w3, yd, hx, out, bw, br):
    step = pl.program_id(0)
    f32, bf = jnp.float32, jnp.bfloat16

    @pl.when(step < NB)
    def _():
        t = t_ref[...]
        for src, dst in ((wave, bw), (resp, br)):
            c = jnp.concatenate([src[0, 0], src[0, 1]], axis=0)
            zb = jnp.dot(t, c, preferred_element_type=f32).astype(bf)
            groups = BL // 384
            for row, w in enumerate((w0, w1, w2, w3)):
                js = sorted({(96 * row) // 128, (96 * row + 95) // 128})
                lhs = jnp.concatenate([
                    jnp.concatenate([zb[96 * s:96 * s + 96, 384 * g + 128 * j:384 * g + 128 * j + 128] for j in js for s in range(2)], axis=1)
                    for g in range(groups)], axis=0)
                res = jnp.dot(lhs, w[...], preferred_element_type=f32)
                for g in range(groups):
                    base = step * (BL // 96 * 96) + (4 * g + row) * 96
                    for r in range(2):
                        dst[r, pl.ds(pl.multiple_of(base, 96), 96), :] = res[96 * g:96 * g + 96, 128 * r:128 * r + 128]

    @pl.when(step >= NB)
    def _():
        chunk = step - NB
        weight = occ[idx[0]].astype(f32) * (1.0 / 256.0)

        def body(i, carry):
            t = t_ref[...]
            spaces = []
            for src in (bw, br):
                parts = []
                for q in range(4):
                    z = chunk * 32 + 8 * q + i
                    parts.append(jnp.concatenate([src[r, pl.ds(z, 96, stride=96), :].astype(bf) for r in range(2)], axis=0))
                spaces.append(jnp.dot(t, jnp.concatenate(parts, axis=1), preferred_element_type=f32))
            a, b = spaces
            rho = (a[:96] * b[:96] + a[96:] * b[96:]) * weight
            hi = rho.astype(bf)
            lo = (rho - hi.astype(f32)).astype(bf)
            cols = []
            for j in range(3):
                lhs = jnp.concatenate([hi[:, 128 * j:128 * j + 256], lo[:, 128 * j:128 * j + 256]], axis=1)
                cols.append(jnp.dot(lhs, yd[j], preferred_element_type=f32))
            r = jnp.concatenate(cols, axis=1)
            rhi = r.astype(bf)
            rlo = (r - rhi.astype(f32)).astype(bf)
            g = jnp.dot(hx[...], jnp.concatenate([rhi, rlo], axis=0), preferred_element_type=f32)
            for j in range(3):
                out[j, pl.ds(i, 96, stride=8), :] = g[:, 128 * j:128 * j + 128]
            return carry
        lax.fori_loop(0, 8, body, 0)

def run_a(wave, resp, occ, idx):
    t, hu = np_tables()
    bf = jnp.bfloat16
    ws = [jnp.asarray(w, bf) for w in y_tables(t)]
    yd = dense_tables(hu)
    yd = jnp.asarray(np.concatenate([yd, yd], axis=1), bf)
    hx = jnp.asarray(np.concatenate([hu, hu], axis=1), bf)
    tb = jnp.asarray(t, bf)
    full = lambda a: pl.BlockSpec(a.shape, lambda i: (0,) * a.ndim)
    consts = [tb, *ws, yd, hx]
    return pl.pallas_call(
        kernel_a,
        grid=(NB + 3,),
        out_shape=jax.ShapeDtypeStruct((9, 768, 128), jnp.float32),
        in_specs=[pl.BlockSpec(memory_space=pltpu.SMEM), pl.BlockSpec(memory_space=pltpu.SMEM),
                  pl.BlockSpec((1, 2, 96, BL), lambda i: (0, 0, 0, jnp.minimum(i, NB - 1))),
                  pl.BlockSpec((1, 2, 96, BL), lambda i: (0, 0, 0, jnp.minimum(i, NB - 1))),
                  *[full(a) for a in consts]],
        out_specs=pl.BlockSpec((3, 768, 128), lambda i: (jnp.maximum(i - NB, 0), 0, 0)),
        scratch_shapes=[pltpu.VMEM((2, 9216, 128), jnp.float32), pltpu.VMEM((2, 9216, 128), jnp.float32)],
        compiler_params=pltpu.CompilerParams(vmem_limit_bytes=60 * 1024 * 1024),
        name="bands",
    )(occ, idx, wave, resp, *consts)

def window_tables(hu):
    h = hu / np.sqrt(N).astype(np.float64)
    rows = np.array([(12 * zc - 2 + w) % N for zc in range(8) for w in range(16)])
    sel = np.zeros((128, N), np.float32)
    sel[np.arange(128), rows] = 1.0
    hye = np.zeros((128, 128), np.float64)
    cols = (np.arange(128) - 16) % N
    hye[:N] = hu[:, cols] / N
    return h.astype(np.float32), h[rows].astype(np.float32), sel, hye.astype(np.float32)


def exact(a, b):
    return jnp.dot(a, b, precision=lax.Precision.HIGHEST, preferred_element_type=jnp.float32)


def kernel_b(d, g, l, hz, hze, sel, hye, hx, out, pbuf, s, f1, t, f2, zbuf, zs, zr, q, a, gr,
             p_snd, p_rcv, s1, r1, s2, r2, sz, rz, sa, ra, sg, rg):
    pool, slab = lax.axis_index("pool"), lax.axis_index("slab")
    y, x = pool // 4, pool % 4
    zc, core = slab // 2, slab % 2
    other = 1 - core
    partner = zc * 2 + other

    def dev(p, sl):
        return {"pool": p, "slab": sl}

    def plane(k):
        dc, dp = k // 16, k % 16
        c2 = (core + dc) % 2
        return c2, dev((pool + dp) % 16, zc * 2 + c2)

    barrier = pltpu.get_barrier_semaphore()
    def hail(who):
        pl.semaphore_signal(barrier, inc=1, device_id=who, device_id_type=MESH)
    for k in range(1, 32):
        hail(plane(k)[1])
    for dz in range(1, 8):
        hail(dev(pool, (slab + 2 * dz) % 16))
    hail(dev(pool, (slab + 15 + 2 * core) % 16))
    pl.semaphore_wait(barrier, 39)

    def send(src, dst, ssem, rsem, who):
        cp = pltpu.make_async_remote_copy(src_ref=src, dst_ref=dst, send_sem=ssem, recv_sem=rsem, device_id=who, device_id_type=MESH)
        cp.start()
        return cp

    pair = [send(d.at[u, other], pbuf.at[u], p_snd.at[u], p_rcv.at[u], dev(pool, partner)) for u in range(9)]
    gs = [send(g, gr.at[0], sg.at[0], rg.at[0], dev(pool, (slab + 1) % 16)),
          send(g, gr.at[1], sg.at[1], rg.at[1], dev(pool, (slab + 15) % 16))]

    first = []
    for u in range(9):
        pair[u].wait_recv()
        s[u] = d[u, core] + pbuf[u]
        cps = []
        for k in range(1, 4):
            if u % 2 == 0:
                o = (x + k) % 4
                cps.append(send(s.at[u, :, o], f1.at[u, k - 1], s1.at[u, k - 1], r1.at[u, k - 1], dev(y * 4 + o, slab)))
            else:
                o = (y + k) % 4
                cps.append(send(s.at[u, o], f1.at[u, k - 1], s1.at[u, k - 1], r1.at[u, k - 1], dev(o * 4 + x, slab)))
        first.append(cps)

    second = []
    for u in range(9):
        for cp in first[u]:
            cp.wait_recv()
        own = s[u, :, x] if u % 2 == 0 else s[u, y]
        t[u] = own + f1[u, 0] + f1[u, 1] + f1[u, 2]
        cps = []
        for k in range(1, 4):
            if u % 2 == 0:
                o = (y + k) % 4
                who = dev(o * 4 + x, slab)
            else:
                o = (x + k) % 4
                who = dev(y * 4 + o, slab)
            cps.append(send(t.at[u, o], f2.at[u, k - 1], s2.at[u, k - 1], r2.at[u, k - 1], who))
        second.append(cps)

    lane = lax.broadcasted_iota(jnp.int32, (8, 128), 1)
    for c in range(3):
        parts = []
        for j in range(3):
            u = 3 * c + j
            for cp in second[u]:
                cp.wait_recv()
            own = t[u, y] if u % 2 == 0 else t[u, x]
            parts.append(own + f2[u, 0] + f2[u, 1] + f2[u, 2])
        for m in range(3):
            v = jnp.concatenate([parts[j][m] for j in range(3)], axis=1)
            for k in range(4):
                w = v if k == 0 else pltpu.roll(v, 384 - 96 * k, 1)
                zbuf[32 * c + 8 * k:32 * c + 8 * k + 8, 128 * m:128 * m + 128] = jnp.where(lane < 96, w[:, :128], 0.0)

    zk = zbuf[...]
    vh = exact(hz[...], zk)
    kz = lax.broadcasted_iota(jnp.int32, (96, 128), 0)
    ky = lax.broadcasted_iota(jnp.int32, (96, 128), 1)
    qz = jnp.where(2 * kz >= N, kz - N, kz)
    qy = jnp.where(2 * ky >= N, ky - N, ky)
    zy = qz * qz + qy * qy
    scaled = []
    for m in range(3):
        kx = jnp.full((96, 128), 1, jnp.int32) * (3 * (core * 16 + pool) + m)
        qx = jnp.where(2 * kx >= N, kx - N, kx)
        squared = (zy + qx * qx).astype(jnp.float32) * ((full_turn / N) ** 2)
        kernel = jnp.where(squared > 0, full_turn / jnp.where(squared > 0, squared, 1.0), 0.0)
        scaled.append(vh[:, 128 * m:128 * m + 128] * kernel)
    vz = exact(hze[...], jnp.concatenate(scaled, axis=1))
    dz_ = exact(sel[...], zk)
    rows = jnp.concatenate([dz_[:, :128], dz_[:, 128:256], dz_[:, 256:], vz[:, :128], vz[:, 128:256], vz[:, 256:]], axis=0)
    both = exact(rows, hye[...])
    for b in range(6):
        for zd in range(8):
            zs[zd, b] = both[128 * b + 16 * zd:128 * b + 16 * zd + 16]

    zcp = []
    for k in range(1, 8):
        o = (zc + k) % 8
        zcp.append(send(zs.at[o], zr.at[k - 1], sz.at[k - 1], rz.at[k - 1], dev(pool, o * 2 + core)))
    f = zs[zc]
    for k in range(7):
        zcp[k].wait_recv()
        f = f + zr[k]
    for c2 in range(2):
        for m in range(3):
            q[c2, m] = jnp.concatenate([f[m][6 * c2:6 * c2 + 10], f[3 + m][6 * c2 + 2:6 * c2 + 8]], axis=0)
    me = 3 * (core * 16 + pool)
    acp = []
    for k in range(1, 32):
        c2, who = plane(k)
        acp.append(send(q.at[c2], a.at[pl.ds(me, 3)], sa.at[k - 1], ra.at[k - 1], who))
    a[pl.ds(me, 3)] = q[core]
    for cp in acp:
        cp.wait_recv()
    for cp in gs:
        cp.wait_recv()

    def turn(kx, acc):
        blk = a[kx]
        return tuple(acc[i] + hx[((6 * pool + 94 + i) % 96) * 96 + kx] * blk for i in range(10))
    acc = lax.fori_loop(0, 96, turn, tuple(jnp.zeros((16, 128), jnp.float32) for _ in range(10)))

    across = []
    for i in range(8):
        across.append(g[i][0:6] * ((acc[i + 2][2:8] - acc[i][2:8]) * 0.5))
    for i in range(6):
        rho = acc[i + 2]
        coef = g[i + 1]
        gz = jnp.concatenate([gr[0, i + 1][5:6], coef[0:6], gr[1, i + 1][0:1]], axis=0)
        flux = gz * ((rho[2:10] - rho[0:8]) * 0.5)
        div = (flux[2:8] - flux[0:6]) * 0.5
        div = div + (across[i + 2] - across[i]) * 0.5
        slope = (pltpu.roll(rho, 127, 1) - pltpu.roll(rho, 1, 1)) * 0.5
        along = coef * slope[2:10]
        div = div + ((pltpu.roll(along, 127, 1) - pltpu.roll(along, 1, 1)) * 0.5)[0:6]
        out[i, 0:6, :] = rho[10:16] + l[i][0:6] * rho[2:8] - div
        out[i, 6:8, :] = jnp.zeros((2, 128), jnp.float32)

    for cps in [pair, gs, *first, *second, zcp, acp]:
        for cp in cps:
            cp.wait_send()


def run_b(d, g, l):
    _, hu = np_tables()
    tabs = [jnp.asarray(a) for a in window_tables(hu)]
    hx = jnp.asarray((hu / N).astype(np.float32).reshape(-1))
    f32 = jnp.float32
    vm = pl.BlockSpec(memory_space=pltpu.VMEM)
    dma = pltpu.SemaphoreType.DMA
    return pl.pallas_call(
        kernel_b,
        out_shape=jax.ShapeDtypeStruct((6, 8, 128), f32),
        in_specs=[vm] * 7 + [pl.BlockSpec(memory_space=pltpu.SMEM)],
        out_specs=vm,
        scratch_shapes=[
            pltpu.VMEM((9, 4, 4, 3, 8, 128), f32), pltpu.VMEM((9, 4, 4, 3, 8, 128), f32),
            pltpu.VMEM((9, 3, 4, 3, 8, 128), f32), pltpu.VMEM((9, 4, 3, 8, 128), f32),
            pltpu.VMEM((9, 3, 3, 8, 128), f32), pltpu.VMEM((96, 384), f32),
            pltpu.VMEM((8, 6, 16, 128), f32), pltpu.VMEM((7, 6, 16, 128), f32),
            pltpu.VMEM((2, 3, 16, 128), f32), pltpu.VMEM((96, 16, 128), f32), pltpu.VMEM((2, 8, 8, 128), f32),
            dma((9,)), dma((9,)), dma((9, 3)), dma((9, 3)), dma((9, 3)), dma((9, 3)), dma((7,)), dma((7,)),
            dma((31,)), dma((31,)), dma((2,)), dma((2,)),
        ],
        compiler_params=pltpu.CompilerParams(collective_id=0, has_side_effects=True, vmem_limit_bytes=60 * 1024 * 1024),
        name="gather",
    )(d, g, l, *tabs, hx)


def rows_of(kernel3, first, count):
    wide = jnp.concatenate([kernel3[:, 95:], kernel3, kernel3[:, :1]], axis=1)
    part = jnp.transpose(lax.dynamic_slice_in_dim(wide, first + 1, count, 1), (1, 0, 2))
    part = jnp.concatenate([part[..., 80:], part, part[..., :16]], axis=2)
    return jnp.pad(part, ((0, 0), (0, 2), (0, 0)))


def shards(wave_coeff, response_coeff, band_index, occupation, local_kernel, gradient_kernel):
    d = run_a(wave_coeff, response_coeff, occupation, band_index)
    row = 6 * lax.axis_index("pool")
    g = rows_of(gradient_kernel.reshape(6, N, N), row - 1, 8)
    l = rows_of(local_kernel.reshape(6, N, N), row, 6)
    res = run_b(d.reshape(9, 2, 4, 4, 3, 8, 128), g, l)
    return jnp.transpose(res[:, :6, 16:112], (1, 0, 2)).reshape(6, 576)


def solution(mesh):
    return jax.shard_map(
        shards,
        mesh=mesh,
        in_specs=(
            P(("pool", "slab"), None, None, None),
            P(("pool", "slab"), None, None, None),
            P(("pool", "slab")),
            P(),
            P("slab", None),
            P("slab", None),
        ),
        out_specs=P("slab", "pool"),
        check_vma=False,
    )
```

time: 242 us -> 99.8 us (0.41)
  Pallas kernels: 0 us -> 93.1 us
  starting transfers between devices: 68.9 us -> 0 us
  local copies, waits for them, and re-layouts: 47.3 us -> 4.2 us
  blocking collectives: 40.3 us -> 0 us
  waiting for transfers between devices: 33.9 us -> 0 us
  matrix products: 33.4 us -> 0 us
  other arithmetic: 14.9 us -> 1.43 us
    pallas_call x0 -> x2, Pallas kernels: none -> 93.1 us  [the longest x1 59.8 us: run_b(): pl.pallas_call(kernel_b, out_shape=jax.ShapeDtypeStruct((6, 8, 128), f32)...]
    unnamed x1 -> x0, blocking collectives: 40.3 us -> none
    all_to_all x5 -> x0, starting transfers between devices: 37.2 us -> none  [the longest x1 15.4 us: shards(): lax.all_to_all(across_done, 'slab', split_axis=2, concat_axis=1, tiled=True)]
    all_to_all x5 -> x0, waiting for transfers between devices: 33.7 us -> none  [the longest x1 7.81 us: sent_and_summed(): parts = lax.all_to_all(split_up(array, dim, length), axis, 0, 0, tiled=True)]
    dot_general x10 -> x0, matrix products: 33.4 us -> none  [the longest x4 31.5 us: half_pass(): return jnp.einsum(spec, tables, values, preferred_element_type=jnp.float32)]
    ppermute x8 -> x0, starting transfers between devices: 16.8 us -> none  [the longest x4 9.08 us: padded_2(): lax.ppermute(last, axis, up)]
    unnamed x36 -> x0, local copies, waits for them, and re-layouts: 15.9 us -> none
    another operation x3 -> x0, local copies, waits for them, and re-layouts: 15.8 us -> none
  transfers between devices with their start and end apart: 17 -> 0, of which waited for: 6 -> 0; matrix products, arithmetic and copies ran while one was open for 9% -> 0% of each run, Pallas kernels for 0% -> 0%
where the time goes in v1:
time: 99.8 us; the launch traced here: 99.5 us
  Pallas kernels  93.1 us (93%)
  local copies, waits for them, and re-layouts  4.2 us (4%)
  other arithmetic  1.43 us (1%)
    pallas_call x1, Pallas kernels, run_b(): pl.pallas_call(kernel_b, out_shape=jax.ShapeDtypeStruct((6, 8, 128), f32)...  59.8 us
    pallas_call x1, Pallas kernels, run_a(): pl.pallas_call(kernel_a, grid=(NB + 3,), out_shape=jax.ShapeDtypeStruct((...  33.3 us

profile of v1, /device:TPU:1, one launch (start us, length us, event | category | flops | bytes accessed | tf_op | source)
XLA Modules:
  0.0 99.5 jit_solution(6586995222628452792)
XLA Ops:
  0.7 1.1 %reshape.14 = f32[6,96,96]{2,1,0:T(8,128)S(1)} reshape(f32[6,9216]{1,0:T(8,128)} %param.22) | data formatting | bytes 442368 | tf_op jit(solution)/shard_map/reshape | solution.py:332
  1.7 0.2 copy.22
  2.0 0.1 fusion.9
  2.1 0.7 select_maximum_fusion.2.l
  2.7 1.1 %reshape.13 = f32[6,96,96]{2,1,0:T(8,128)S(1)} reshape(f32[6,9216]{1,0:T(8,128)} %param.23) | data formatting | bytes 442368 | tf_op jit(solution)/shard_map/reshape | solution.py:331
  3.8 0.2 copy.19
  4.1 0.1 fusion.8
  4.1 0.7 select_maximum_fusion.g
  4.8 33.3 %bands.1 = f32[9,768,128]{2,1,0:T(8,128)} custom-call(s32[256]{0:T(256)} %occ.1, s32[1]{0:T(128)S(6)} %copy.26.idx, bf16[1,2,96,9216]{3,2,1,0:T(8,128)(2,1)} %wave.1, bf16[1,2,96,9216]{3,2,1,0:T(8,128)(2,1)} %resp.1, bf16[192,192]{1,0:T(8,128)(2,1)} %constant.51.clone.t_ref, bf16[256,256]{1,0:T(8,128)(2,1)} %constant.45.clone.w0, ...), custom_call_target="tpu_custom_call" | custom-call | tf_op jit(solution)/shard_map/bands/pallas_call | solution.py:115
  38.1 59.8 %gather.1 = f32[6,8,128]{2,1,0:T(8,128)} custom-call(f32[9,2,4,4,3,8,128]{6,5,4,3,2,1,0:T(8,128)} %bitcast.7, f32[8,8,128]{2,1,0:T(8,128)} %select_maximum_fusion.g, f32[6,8,128]{2,1,0:T(8,128)} %select_maximum_fusion.2.l, f32[96,96]{1,0:T(8,128)} %constant.52.clone.hz, f32[128,96]{1,0:T(8,128)} %constant.53.clone.hze, f32[128,96]{1,0:T(8,128)} %constant.54.clone.sel, ...), custom_call_target="tpu_custom_call" | custom-call | tf_op jit(solution)/shard_map/gather/pallas_call | solution.py:302
  97.9 0.8 slice_bitcast_fusion
  98.8 0.7 reshape.15
  (5 shorter events, 0.1 us)

commit v2 on v0

v2 whole, which is shorter than its diff:
```python
import math

import numpy as np
import jax
import jax.numpy as jnp
from jax import lax
from jax.experimental import pallas as pl
from jax.experimental.pallas import tpu as pltpu
from jax.sharding import PartitionSpec as P

MESH = pl.DeviceIdType.MESH
full_turn = 2.0 * math.pi
N = 96
BL = 1536
NB = 9216 // BL


def np_tables():
    k = np.arange(N)
    ang = (np.outer(k, k) % N) * (2 * np.pi / N)
    c, s = np.cos(ang) / np.sqrt(N), np.sin(ang) / np.sqrt(N)
    t = np.block([[c, -s], [s, c]])
    return t, np.cos(ang) + np.sin(ang)


def y_tables(t):
    outs = []
    for row in range(4):
        js = sorted({(96 * row) // 128, (96 * row + 95) // 128})
        w = np.zeros((256 * len(js), 256))
        for n, j in enumerate(js):
            for l in range(128):
                d = 128 * j + l
                if d // 96 != row:
                    continue
                for s in range(2):
                    for r in range(2):
                        w[256 * n + 128 * s + l, 128 * r:128 * r + 96] = t[96 * r:96 * r + 96, 96 * s + d % 96]
        outs.append(w)
    return outs


def dense_tables(hu):
    outs = []
    for j in range(3):
        w = np.zeros((256, 128))
        for l in range(128):
            q, ky = divmod(128 * j + l, 96)
            w[(q - j) * 128:(q - j) * 128 + 96, l] = hu[ky]
        outs.append(np.concatenate([w, w], axis=0))
    return np.stack(outs)


def window_tables(hu):
    h = hu / math.sqrt(N)
    rows = np.array([(12 * zc - 2 + w) % N for zc in range(8) for w in range(16)])
    sel = np.zeros((128, N))
    sel[np.arange(128), rows] = 1.0
    hye = np.zeros((128, 128))
    hye[:N] = hu[:, (np.arange(128) - 16) % N] / N
    return [h, h[rows], sel, hye]


def x_table(hu):
    w = np.zeros((16, 16, 32, 8))
    for p in range(16):
        for i in range(10):
            w[p, i, :, :3] = (hu[(6 * p - 2 + i) % N] / N).reshape(32, 3)
    w = w.reshape(256, 256)
    hi = w.astype(jnp.bfloat16).astype(np.float64)
    return np.concatenate([hi, hi, w - hi], axis=1)


def exact(a, b):
    return jnp.dot(a, b, precision=lax.Precision.HIGHEST, preferred_element_type=jnp.float32)


def halves(v):
    hi = v.astype(jnp.bfloat16)
    return hi, (v - hi.astype(jnp.float32)).astype(jnp.bfloat16)


def swap(t):
    return t + 1 - 2 * (t % 2)


def mirror(t):
    return 3 - t


def kernel(occ, idx, wave, resp, g, l, t_ref, w0, w1, w2, w3, yd, hx, hz, hze, sel, hye, hxe, out,
           cw, cr, bw, br, d, pbuf, s, f1, t1, f2, t2, f3, u1, f4, zbuf, zs, zrel, zr, q, a, xo, b, gr,
           csem, p_snd, p_rcv, s1, r1, s2, r2, s3, r3, s4, r4, sz, rz, sa, ra, sb, rb, sg, rg):
    f32, bf = jnp.float32, jnp.bfloat16
    pool, slab = lax.axis_index("pool"), lax.axis_index("slab")
    y, x = pool // 4, pool % 4
    zc, core = slab // 2, slab % 2
    other = 1 - core

    def load(k, blk):
        return pltpu.make_async_copy((wave, resp)[k].at[0, :, :, pl.ds(pl.multiple_of(blk * BL, BL), BL)], (cw, cr)[k].at[blk], csem.at[k, blk])

    for blk in range(NB):
        for k in range(2):
            load(k, blk).start()

    def dev(p, sl):
        return {"pool": p, "slab": sl}

    def plane(k):
        dc, dp = k // 16, k % 16
        c2 = (core + dc) % 2
        p2 = (pool + dp) % 16
        return c2, p2, dev(p2, zc * 2 + c2)

    barrier = pltpu.get_barrier_semaphore()

    def hail(who):
        pl.semaphore_signal(barrier, inc=1, device_id=who, device_id_type=MESH)

    for k in range(1, 32):
        hail(plane(k)[2])
    for dz in (1, 2, 3, 5, 6, 7):
        hail(dev(pool, (slab + 2 * dz) % 16))
    hail(dev(pool, (slab + 15 + 2 * core) % 16))

    def send(src, dst, ssem, rsem, who):
        cp = pltpu.make_async_remote_copy(src_ref=src, dst_ref=dst, send_sem=ssem, recv_sem=rsem, device_id=who, device_id_type=MESH)
        cp.start()
        return cp

    q[...] = jnp.zeros_like(q)

    def first_phase(blk, carry):
        for k in range(2):
            load(k, blk).wait()
        t = t_ref[...]
        for src, dst in ((cw, bw), (cr, br)):
            c = jnp.concatenate([src[blk, 0], src[blk, 1]], axis=0)
            zb = jnp.dot(t, c, preferred_element_type=f32).astype(bf)
            groups = BL // 384
            for row, w in enumerate((w0, w1, w2, w3)):
                js = sorted({(96 * row) // 128, (96 * row + 95) // 128})
                lhs = jnp.concatenate([
                    jnp.concatenate([zb[96 * r:96 * r + 96, 384 * n + 128 * j:384 * n + 128 * j + 128] for j in js for r in range(2)], axis=1)
                    for n in range(groups)], axis=0)
                res = jnp.dot(lhs, w[...], preferred_element_type=f32)
                for n in range(groups):
                    base = pl.multiple_of(blk * BL + (4 * n + row) * 96, 96)
                    for r in range(2):
                        dst[r, pl.ds(base, 96), :] = res[96 * n:96 * n + 96, 128 * r:128 * r + 128]
        return carry

    weight = occ[idx[0]].astype(f32) * (1.0 / 256.0)

    def second_phase(chunk, first, last):
        def body(i, carry):
            t = t_ref[...]
            spaces = []
            for src in (bw, br):
                parts = []
                for k in range(4):
                    z = chunk * 32 + 8 * k + i
                    parts.append(jnp.concatenate([src[r, pl.ds(z, 96, stride=96), :].astype(bf) for r in range(2)], axis=0))
                spaces.append(jnp.dot(t, jnp.concatenate(parts, axis=1), preferred_element_type=f32))
            v, w = spaces
            rho = (v[:96] * w[:96] + v[96:] * w[96:]) * weight
            hi, lo = halves(rho)
            cols = []
            for j in range(3):
                lhs = jnp.concatenate([hi[:, 128 * j:128 * j + 256], lo[:, 128 * j:128 * j + 256]], axis=1)
                cols.append(jnp.dot(lhs, yd[j], preferred_element_type=f32))
            gx = jnp.dot(hx[...], jnp.concatenate(halves(jnp.concatenate(cols, axis=1)), axis=0), preferred_element_type=f32)
            for j in range(3):
                d[3 * chunk + j, pl.ds(i, 96, stride=8), :] = gx[:, 128 * j:128 * j + 128]
            return carry
        lax.fori_loop(first, last, body, 0)

    log = {}

    def variant(u):
        return (u % 4) % 2, (u % 4) // 2

    def order(u, along):
        ax, par = variant(u)
        pos = (x, y)[(ax + along) % 2]
        p1, p2 = (swap, mirror) if par == 0 else (mirror, swap)
        return pos, p1, p2, (ax + along) % 2

    def at(ax, pos):
        return dev(y * 4 + pos, slab) if ax == 0 else dev(pos * 4 + x, slab)

    def units(c):
        return range(3 * c, 3 * c + 3)

    def start_pair(c):
        for u in units(c):
            log["p", u] = send(d.at[u, pl.ds(pl.multiple_of(other * 384, 384), 384)], pbuf.at[u], p_snd.at[u], p_rcv.at[u], dev(pool, zc * 2 + other))

    def start_a1(c):
        for u in units(c):
            log["p", u].wait_recv()
            s[u] = (d[u, pl.ds(pl.multiple_of(core * 384, 384), 384), :] + pbuf[u]).reshape(4, 4, 3, 8, 128)
            pos, p1, p2, ax = order(u, 0)
            to = p1(pos)
            for n, blk in enumerate((to, p2(to))):
                src = s.at[u, :, blk] if ax == 0 else s.at[u, blk]
                log["a1", u, n] = send(src, f1.at[u, n], s1.at[u, n], r1.at[u, n], at(ax, to))

    def start_a2(c):
        for u in units(c):
            pos, p1, p2, ax = order(u, 0)
            for n, blk in ((1, p2(pos)), (0, pos)):
                log["a1", u, n].wait_recv()
                own = s[u, :, blk] if ax == 0 else s[u, blk]
                t1[u, n] = own + f1[u, n]
                if n == 1:
                    log["a2", u] = send(t1.at[u, 1], f2.at[u], s2.at[u], r2.at[u], at(ax, p2(pos)))

    def start_b1(c):
        for u in units(c):
            log["a2", u].wait_recv()
            t2[u] = t1[u, 0] + f2[u]
            pos, p1, p2, ax = order(u, 1)
            to = p1(pos)
            for n, blk in enumerate((to, p2(to))):
                log["b1", u, n] = send(t2.at[u, blk], f3.at[u, n], s3.at[u, n], r3.at[u, n], at(ax, to))

    def start_b2(c):
        for u in units(c):
            pos, p1, p2, ax = order(u, 1)
            for n, blk in ((1, p2(pos)), (0, pos)):
                log["b1", u, n].wait_recv()
                u1[u, n] = t2[u, blk] + f3[u, n]
                if n == 1:
                    log["b2", u] = send(u1.at[u, 1], f4.at[u], s4.at[u], r4.at[u], at(ax, p2(pos)))

    lane = lax.broadcasted_iota(jnp.int32, (8, 128), 1)

    def finish(c):
        parts = []
        for u in units(c):
            log["b2", u].wait_recv()
            parts.append(u1[u, 0] + f4[u])
        for m in range(3):
            v = jnp.concatenate([parts[j][m] for j in range(3)], axis=1)
            for k in range(4):
                w = v if k == 0 else pltpu.roll(v, 384 - 96 * k, 1)
                zbuf[32 * c + 8 * k:32 * c + 8 * k + 8, 128 * m:128 * m + 128] = jnp.where(lane < 96, w[:, :128], 0.0)

    with jax.named_scope("first_phase"):
        lax.fori_loop(0, NB, first_phase, 0)
    with jax.named_scope("chunk0"):
        second_phase(0, 0, 8)
    with jax.named_scope("barrier"):
        pl.semaphore_wait(barrier, 38)
    start_pair(0)
    gs = [send(g.at[5], gr.at[0], sg.at[0], rg.at[0], dev(pool, (slab + 1) % 16)),
          send(g.at[0], gr.at[1], sg.at[1], rg.at[1], dev(pool, (slab + 15) % 16))]
    with jax.named_scope("chunk1a"):
        second_phase(1, 0, 4)
    with jax.named_scope("comm1a"):
        start_a1(0)
    with jax.named_scope("chunk1b"):
        second_phase(1, 4, 8)
    with jax.named_scope("comm1b"):
        start_pair(1)
        start_a2(0)
    with jax.named_scope("chunk2a"):
        second_phase(2, 0, 4)
    with jax.named_scope("comm2a"):
        start_a1(1)
        start_b1(0)
    with jax.named_scope("chunk2b"):
        second_phase(2, 4, 8)
    with jax.named_scope("comm2b"):
        start_pair(2)
        start_a2(1)
        start_b2(0)
    with jax.named_scope("tail_a1"):
        start_a1(2)
        start_b1(1)
        finish(0)
    with jax.named_scope("tail_a2"):
        start_a2(2)
        start_b2(1)
    with jax.named_scope("tail_b1"):
        start_b1(2)
        finish(1)
    with jax.named_scope("tail_b2"):
        start_b2(2)
    with jax.named_scope("tail_end"):
        finish(2)

    with jax.named_scope("solve"):
        zk = zbuf[...]
        vh = exact(hz[...], zk)
        kz = lax.broadcasted_iota(jnp.int32, (96, 128), 0)
        ky = lax.broadcasted_iota(jnp.int32, (96, 128), 1)
        qz = jnp.where(2 * kz >= N, kz - N, kz)
        qy = jnp.where(2 * ky >= N, ky - N, ky)
        zy = qz * qz + qy * qy
        scaled = []
        for m in range(3):
            kx = jnp.full((96, 128), 1, jnp.int32) * (3 * (core * 16 + pool) + m)
            qx = jnp.where(2 * kx >= N, kx - N, kx)
            squared = (zy + qx * qx).astype(f32) * ((full_turn / N) ** 2)
            screen = jnp.where(squared > 0, full_turn / jnp.where(squared > 0, squared, 1.0), 0.0)
            scaled.append(vh[:, 128 * m:128 * m + 128] * screen)
        vz = exact(hze[...], jnp.concatenate(scaled, axis=1))
        rz_ = exact(sel[...], zk)
        rows = jnp.concatenate([v[:, 128 * m:128 * m + 128] for v in (rz_, vz) for m in range(3)], axis=0)
        both = exact(rows, hye[...])
        for n in range(6):
            for zd in range(8):
                zs[zd, n] = both[128 * n + 16 * zd:128 * n + 16 * zd + 16]

    with jax.named_scope("zstage"):
        def col(k):
            return dev(pool, ((zc + k) % 8) * 2 + core)
        relay = send(zs.at[(zc + 4) % 8], zrel.at[0], sz.at[0], rz.at[0], col(7))
        zcp = [send(zs.at[(zc + k) % 8], zr.at[k - 1], sz.at[k], rz.at[k], col(k)) for k in (3, 6, 2, 7, 1)]
        relay.wait_recv()
        zrel[1] = zs[(zc + 5) % 8] + zrel[0]
        zcp.append(send(zrel.at[1], zr.at[4], sz.at[5], rz.at[5], col(5)))
        f = zs[zc]
        for cp, k in zip(reversed(zcp[:-1]), (1, 7, 2, 6, 3)):
            cp.wait_recv()
            f = f + zr[k - 1]
        zcp[-1].wait_recv()
        f = f + zr[4]

    with jax.named_scope("rows_out"):
        for c2 in range(2):
            for m in range(3):
                base = c2 * 128 + m
                q[pl.ds(base, 10, stride=8), :] = f[m][6 * c2:6 * c2 + 10]
                q[pl.ds(base + 80, 6, stride=8), :] = f[3 + m][6 * c2 + 2:6 * c2 + 8]
        me = core * 16 + pool

        def row(c2, p2):
            return pl.ds(pl.multiple_of((c2 * 16 + p2) * 8, 8), 8)
        mine = pl.ds(pl.multiple_of(me * 8, 8), 8)
        acp = []
        for k in range(1, 32):
            c2, p2, who = plane(k)
            acp.append(send(q.at[row(c2, p2)], a.at[mine], sa.at[k - 1], ra.at[k - 1], who))
        a[mine, :] = q[row(core, pool), :]
        for cp in acp:
            cp.wait_recv()
    with jax.named_scope("rows_back"):
        hi, lo = halves(a[...])
        xo[...] = jnp.dot(hxe[...], jnp.concatenate([hi, lo, hi], axis=0), preferred_element_type=f32).reshape(16, 16, 128)
        bcp = []
        for k in range(1, 16):
            p2 = (pool + k) % 16
            bcp.append(send(xo.at[p2], b.at[pool], sb.at[k - 1], rb.at[k - 1], dev(p2, slab)))
        b[pool] = xo[pool]
        for cp in gs:
            cp.wait_recv()
        for cp in bcp:
            cp.wait_recv()

    with jax.named_scope("final"):
        def up(v, ax):
            return pltpu.roll(v, v.shape[ax] - 1, ax)

        def down(v, ax):
            return pltpu.roll(v, 1, ax)
        flux = []
        for n in range(8):
            coef = gr[0] if n == 0 else gr[1] if n == 7 else g[n - 1]
            flux.append(coef * ((b[n + 2] - b[n]) * 0.5))
        for n in range(6):
            rho, coef = b[n + 2], g[n]
            div = (flux[n + 2] - flux[n]) * 0.5
            for ax in (0, 1):
                slope = coef * ((up(rho, ax) - down(rho, ax)) * 0.5)
                div = div + (up(slope, ax) - down(slope, ax)) * 0.5
            out[n] = b[10 + n] + l[n] * rho - div

    for cp in [*log.values(), *gs, relay, *zcp, *acp, *bcp]:
        cp.wait_send()


def run(wave, resp, occ, idx, g, l):
    t, hu = np_tables()
    f32, bf = jnp.float32, jnp.bfloat16
    consts = [jnp.asarray(v, bf) for v in (t, *y_tables(t), dense_tables(hu), np.concatenate([hu, hu], axis=1))]
    consts += [jnp.asarray(v, f32) for v in window_tables(hu)]
    consts.append(jnp.asarray(x_table(hu), bf))
    vm, sm, hbm = (pl.BlockSpec(memory_space=m) for m in (pltpu.VMEM, pltpu.SMEM, pl.ANY))
    dma = pltpu.SemaphoreType.DMA
    buf = lambda *dims: pltpu.VMEM(dims, f32)
    return pl.pallas_call(
        kernel,
        out_shape=jax.ShapeDtypeStruct((6, 16, 128), f32),
        in_specs=[sm, sm, hbm, hbm, vm, vm] + [vm] * len(consts),
        out_specs=vm,
        scratch_shapes=[
            pltpu.VMEM((NB, 2, 96, BL), bf), pltpu.VMEM((NB, 2, 96, BL), bf),
            buf(2, 9216, 128), buf(2, 9216, 128), buf(9, 768, 128), buf(9, 384, 128), buf(9, 4, 4, 3, 8, 128),
            buf(9, 2, 4, 3, 8, 128), buf(9, 2, 4, 3, 8, 128), buf(9, 4, 3, 8, 128), buf(9, 4, 3, 8, 128),
            buf(9, 2, 3, 8, 128), buf(9, 2, 3, 8, 128), buf(9, 3, 8, 128), buf(96, 384),
            buf(8, 6, 16, 128), buf(2, 6, 16, 128), buf(7, 6, 16, 128), buf(256, 128), buf(256, 128),
            buf(16, 16, 128), buf(16, 16, 128), buf(2, 16, 128),
            dma((2, NB)), dma((9,)), dma((9,)), dma((9, 2)), dma((9, 2)), dma((9,)), dma((9,)), dma((9, 2)), dma((9, 2)),
            dma((9,)), dma((9,)), dma((8,)), dma((8,)), dma((31,)), dma((31,)), dma((15,)), dma((15,)), dma((2,)), dma((2,)),
        ],
        compiler_params=pltpu.CompilerParams(collective_id=0, has_side_effects=True, vmem_limit_bytes=60 * 1024 * 1024),
        name="response",
    )(occ, idx, wave, resp, g, l, *consts)


def rows_of(flat, first):
    grid = flat.reshape(6, N, N)
    wide = jnp.concatenate([grid[:, 94:], grid, grid[:, :10]], axis=1)
    part = lax.dynamic_slice_in_dim(wide, first, 16, 1)
    return jnp.concatenate([part[..., 80:], part, part[..., :16]], axis=2)


def shards(wave_coeff, response_coeff, band_index, occupation, local_kernel, gradient_kernel):
    row = 6 * lax.axis_index("pool")
    res = run(wave_coeff, response_coeff, occupation, band_index, rows_of(gradient_kernel, row), rows_of(local_kernel, row))
    return res[:, 2:8, 16:112].reshape(6, 576)


def solution(mesh):
    return jax.shard_map(
        shards,
        mesh=mesh,
        in_specs=(
            P(("pool", "slab"), None, None, None),
            P(("pool", "slab"), None, None, None),
            P(("pool", "slab")),
            P(),
            P("slab", None),
            P("slab", None),
        ),
        out_specs=P("slab", "pool"),
        check_vma=False,
    )
```

time: 242 us -> 86.1 us (0.36)
  Pallas kernels: 0 us -> 79.5 us
  starting transfers between devices: 68.9 us -> 0 us
  local copies, waits for them, and re-layouts: 47.3 us -> 3.85 us
  blocking collectives: 40.3 us -> 0 us
  waiting for transfers between devices: 33.9 us -> 0 us
  matrix products: 33.4 us -> 0 us
  other arithmetic: 14.9 us -> 1.5 us
    pallas_call x0 -> x1, Pallas kernels: none -> 79.5 us  [run(): pl.pallas_call(kernel, out_shape=jax.ShapeDtypeStruct((6, 16, 128), f32),...]
    unnamed x1 -> x0, blocking collectives: 40.3 us -> none
    all_to_all x5 -> x0, starting transfers between devices: 37.2 us -> none  [the longest x1 15.4 us: shards(): lax.all_to_all(across_done, 'slab', split_axis=2, concat_axis=1, tiled=True)]
    all_to_all x5 -> x0, waiting for transfers between devices: 33.7 us -> none  [the longest x1 7.81 us: sent_and_summed(): parts = lax.all_to_all(split_up(array, dim, length), axis, 0, 0, tiled=True)]
    dot_general x10 -> x0, matrix products: 33.4 us -> none  [the longest x4 31.5 us: half_pass(): return jnp.einsum(spec, tables, values, preferred_element_type=jnp.float32)]
    ppermute x8 -> x0, starting transfers between devices: 16.8 us -> none  [the longest x4 9.08 us: padded_2(): lax.ppermute(last, axis, up)]
    unnamed x36 -> x0, local copies, waits for them, and re-layouts: 15.9 us -> none
    another operation x3 -> x0, local copies, waits for them, and re-layouts: 15.8 us -> none
  transfers between devices with their start and end apart: 17 -> 0, of which waited for: 6 -> 0; matrix products, arithmetic and copies ran while one was open for 9% -> 0% of each run, Pallas kernels for 0% -> 0%
where the time goes in v2:
time: 86.1 us; the launch traced here: 85.5 us
  Pallas kernels  79.5 us (92%)
  local copies, waits for them, and re-layouts  3.85 us (4%)
  other arithmetic  1.5 us (2%)
    pallas_call x1, Pallas kernels, run(): pl.pallas_call(kernel, out_shape=jax.ShapeDtypeStruct((6, 16, 128), f32),...  79.5 us
    reshape x2, local copies, waits for them, and re-layouts, rows_of(): grid = flat.reshape(6, N, N)  2.18 us

profile of v2, /device:TPU:1, one launch (start us, length us, event | category | flops | bytes accessed | tf_op | source)
XLA Modules:
  0.0 85.5 jit_solution(16378507837076158169)
XLA Ops:
  0.0 1.1 %reshape.9 = f32[6,96,96]{2,1,0:T(8,128)S(1)} reshape(f32[6,9216]{1,0:T(8,128)} %param.23) | data formatting | bytes 442368 | tf_op jit(solution)/shard_map/reshape | solution.py:416
  1.1 1.1 %reshape.10 = f32[6,96,96]{2,1,0:T(8,128)S(1)} reshape(f32[6,9216]{1,0:T(8,128)} %param.22) | data formatting | bytes 442368 | tf_op jit(solution)/shard_map/reshape | solution.py:416
  2.2 0.1 fusion.1
  2.3 0.1 fusion.4
  2.4 0.7 pad_maximum_fusion.1.l
  3.1 0.1 fusion.5
  3.2 0.7 pad_maximum_fusion.g
  4.6 79.5 %response.1 = f32[6,16,128]{2,1,0:T(8,128)} custom-call(s32[256]{0:T(256)} %occ.1, s32[1]{0:T(128)S(6)} %copy.19.idx, bf16[1,2,96,9216]{3,2,1,0:T(8,128)(2,1)} %wave.1, bf16[1,2,96,9216]{3,2,1,0:T(8,128)(2,1)} %resp.1, f32[6,16,128]{2,1,0:T(8,128)} %pad_maximum_fusion.g, f32[6,16,128]{2,1,0:T(8,128)} %pad_maximum_fusion.1.l, ...), custom_call_target="tpu_custom_call" | custom-call | tf_op jit(solution)/shard_map/response/pallas_call | solution.py:395
  84.0 0.8 slice.35
  84.9 0.7 reshape.11
  (4 shorter events, 0.0 us)

commit v3 on v2

--- a/solution.py
+++ b/solution.py
@@ -13,6 +13,7 @@
 N = 96
 BL = 1536
 NB = 9216 // BL
+STEP = 97
 
 
 def np_tables():
@@ -88,9 +89,11 @@
     return 3 - t
 
 
-def kernel(occ, idx, wave, resp, g, l, t_ref, w0, w1, w2, w3, yd, hx, hz, hze, sel, hye, hxe, out,
-           cw, cr, bw, br, d, pbuf, s, f1, t1, f2, t2, f3, u1, f4, zbuf, zs, zrel, zr, q, a, xo, b, gr,
-           csem, p_snd, p_rcv, s1, r1, s2, r2, s3, r3, s4, r4, sz, rz, sa, ra, sb, rb, sg, rg):
+def kernel(occ, idx, wave, resp, grad, local, *refs):
+    tables, out, held, refs = refs[:12], refs[12], refs[13:25], refs[25:]
+    (cw, cr, bw, br, d, pbuf, s, f1, t1, f2, t2, f3, zbuf, zs, zr, q, a, xo, b, gr, flat, gl, pot,
+     csem, tsem, gsem, p_snd, p_rcv, s1, r1, s2, r2, s3, r3, sz, rz, sa, ra, sb, rb, sg, rg) = refs
+    t_ref, w0, w1, w2, w3, yd, hx, hz, hze, sel, hye, hxe = held
     f32, bf = jnp.float32, jnp.bfloat16
     pool, slab = lax.axis_index("pool"), lax.axis_index("slab")
     y, x = pool // 4, pool % 4
@@ -100,9 +103,20 @@
     def load(k, blk):
         return pltpu.make_async_copy((wave, resp)[k].at[0, :, :, pl.ds(pl.multiple_of(blk * BL, BL), BL)], (cw, cr)[k].at[blk], csem.at[k, blk])
 
+    early = [pltpu.make_async_copy(tables[n], held[n], tsem.at[n]) for n in range(5)]
+    late = [pltpu.make_async_copy(tables[n], held[n], tsem.at[n]) for n in range(5, 12)]
+    for cp in early:
+        cp.start()
     for blk in range(NB):
         for k in range(2):
             load(k, blk).start()
+    for cp in late:
+        cp.start()
+    grids = []
+    for k, src in enumerate((grad, local)):
+        for n, (lo, to, size) in enumerate(((0, 384, 9216), (9216 - 384, 0, 384), (0, 9600, 384))):
+            grids.append(pltpu.make_async_copy(src.at[:, pl.ds(lo, size)], flat.at[k, :, pl.ds(to, size)], gsem.at[k, n]))
+            grids[-1].start()
 
     def dev(p, sl):
         return {"pool": p, "slab": sl}
@@ -120,7 +134,7 @@
 
     for k in range(1, 32):
         hail(plane(k)[2])
-    for dz in (1, 2, 3, 5, 6, 7):
+    for dz in range(1, 8):
         hail(dev(pool, (slab + 2 * dz) % 16))
     hail(dev(pool, (slab + 15 + 2 * core) % 16))
 
@@ -130,6 +144,10 @@
         return cp
 
     q[...] = jnp.zeros_like(q)
+    for u in range(9):
+        d[u, pl.ds(8, 96, stride=9), :] = jnp.zeros((96, 128), f32)
+    for cp in early:
+        cp.wait()
 
     def first_phase(blk, carry):
         for k in range(2):
@@ -146,7 +164,7 @@
                     for n in range(groups)], axis=0)
                 res = jnp.dot(lhs, w[...], preferred_element_type=f32)
                 for n in range(groups):
-                    base = pl.multiple_of(blk * BL + (4 * n + row) * 96, 96)
+                    base = (blk * (BL // 96) + 4 * n + row) * STEP
                     for r in range(2):
                         dst[r, pl.ds(base, 96), :] = res[96 * n:96 * n + 96, 128 * r:128 * r + 128]
         return carry
@@ -154,25 +172,32 @@
     weight = occ[idx[0]].astype(f32) * (1.0 / 256.0)
 
     def second_phase(chunk, first, last):
-        def body(i, carry):
+        def body(step, carry):
             t = t_ref[...]
-            spaces = []
-            for src in (bw, br):
-                parts = []
-                for k in range(4):
-                    z = chunk * 32 + 8 * k + i
-                    parts.append(jnp.concatenate([src[r, pl.ds(z, 96, stride=96), :].astype(bf) for r in range(2)], axis=0))
-                spaces.append(jnp.dot(t, jnp.concatenate(parts, axis=1), preferred_element_type=f32))
-            v, w = spaces
-            rho = (v[:96] * w[:96] + v[96:] * w[96:]) * weight
-            hi, lo = halves(rho)
+            his, los = [], []
+            for n in range(2):
+                i = 2 * step + n
+                spaces = []
+                for src in (bw, br):
+                    parts = []
+                    for k in range(4):
+                        z = chunk * 32 + 8 * k + i
+                        parts.append(jnp.concatenate([src[r, pl.ds(z, 96, stride=STEP), :].astype(bf) for r in range(2)], axis=0))
+                    spaces.append(jnp.dot(t, jnp.concatenate(parts, axis=1), preferred_element_type=f32))
+                v, w = spaces
+                hi, lo = halves((v[:96] * w[:96] + v[96:] * w[96:]) * weight)
+                his.append(hi)
+                los.append(lo)
+            hi, lo = jnp.concatenate(his, axis=0), jnp.concatenate(los, axis=0)
             cols = []
             for j in range(3):
                 lhs = jnp.concatenate([hi[:, 128 * j:128 * j + 256], lo[:, 128 * j:128 * j + 256]], axis=1)
                 cols.append(jnp.dot(lhs, yd[j], preferred_element_type=f32))
-            gx = jnp.dot(hx[...], jnp.concatenate(halves(jnp.concatenate(cols, axis=1)), axis=0), preferred_element_type=f32)
-            for j in range(3):
-                d[3 * chunk + j, pl.ds(i, 96, stride=8), :] = gx[:, 128 * j:128 * j + 128]
+            cols = jnp.concatenate([col[96 * n:96 * n + 96] for n in range(2) for col in cols], axis=1)
+            gx = jnp.dot(hx[...], jnp.concatenate(halves(cols), axis=0), preferred_element_type=f32)
+            for n in range(2):
+                for j in range(3):
+                    d[3 * chunk + j, pl.ds(2 * step + n, 96, stride=9), :] = gx[:, 384 * n + 128 * j:384 * n + 128 * j + 128]
             return carry
         lax.fori_loop(first, last, body, 0)
 
@@ -195,12 +220,13 @@
 
     def start_pair(c):
         for u in units(c):
-            log["p", u] = send(d.at[u, pl.ds(pl.multiple_of(other * 384, 384), 384)], pbuf.at[u], p_snd.at[u], p_rcv.at[u], dev(pool, zc * 2 + other))
+            log["p", u] = send(d.at[u, pl.ds(pl.multiple_of(other * 432, 432), 432)], pbuf.at[u], p_snd.at[u], p_rcv.at[u], dev(pool, zc * 2 + other))
 
     def start_a1(c):
         for u in units(c):
             log["p", u].wait_recv()
-            s[u] = (d[u, pl.ds(pl.multiple_of(core * 384, 384), 384), :] + pbuf[u]).reshape(4, 4, 3, 8, 128)
+            for n in range(48):
+                s[u, n // 12, n // 3 % 4, n % 3] = d[u, pl.ds(core * 432 + 9 * n, 8), :] + pbuf[u, pl.ds(9 * n, 8), :]
             pos, p1, p2, ax = order(u, 0)
             to = p1(pos)
             for n, blk in enumerate((to, p2(to))):
@@ -217,31 +243,25 @@
                 if n == 1:
                     log["a2", u] = send(t1.at[u, 1], f2.at[u], s2.at[u], r2.at[u], at(ax, p2(pos)))
 
-    def start_b1(c):
+    def start_b(c):
         for u in units(c):
             log["a2", u].wait_recv()
             t2[u] = t1[u, 0] + f2[u]
-            pos, p1, p2, ax = order(u, 1)
-            to = p1(pos)
-            for n, blk in enumerate((to, p2(to))):
-                log["b1", u, n] = send(t2.at[u, blk], f3.at[u, n], s3.at[u, n], r3.at[u, n], at(ax, to))
-
-    def start_b2(c):
-        for u in units(c):
-            pos, p1, p2, ax = order(u, 1)
-            for n, blk in ((1, p2(pos)), (0, pos)):
-                log["b1", u, n].wait_recv()
-                u1[u, n] = t2[u, blk] + f3[u, n]
-                if n == 1:
-                    log["b2", u] = send(u1.at[u, 1], f4.at[u], s4.at[u], r4.at[u], at(ax, p2(pos)))
+            pos, _, _, ax = order(u, 1)
+            for k in (2, 1, 3):
+                to = (pos + k) % 4
+                log["b", u, k] = send(t2.at[u, to], f3.at[u, k - 1], s3.at[u, k - 1], r3.at[u, k - 1], at(ax, to))
 
     lane = lax.broadcasted_iota(jnp.int32, (8, 128), 1)
 
     def finish(c):
         parts = []
         for u in units(c):
-            log["b2", u].wait_recv()
-            parts.append(u1[u, 0] + f4[u])
+            part = t2[u, order(u, 1)[0]]
+            for k in (1, 3, 2):
+                log["b", u, k].wait_recv()
+                part = part + f3[u, k - 1]
+            parts.append(part)
         for m in range(3):
             v = jnp.concatenate([parts[j][m] for j in range(3)], axis=1)
             for k in range(4):
@@ -251,44 +271,40 @@
     with jax.named_scope("first_phase"):
         lax.fori_loop(0, NB, first_phase, 0)
     with jax.named_scope("chunk0"):
-        second_phase(0, 0, 8)
+        for cp in late:
+            cp.wait()
+        second_phase(0, 0, 4)
     with jax.named_scope("barrier"):
-        pl.semaphore_wait(barrier, 38)
+        pl.semaphore_wait(barrier, 39)
     start_pair(0)
-    gs = [send(g.at[5], gr.at[0], sg.at[0], rg.at[0], dev(pool, (slab + 1) % 16)),
-          send(g.at[0], gr.at[1], sg.at[1], rg.at[1], dev(pool, (slab + 15) % 16))]
     with jax.named_scope("chunk1a"):
-        second_phase(1, 0, 4)
+        second_phase(1, 0, 2)
     with jax.named_scope("comm1a"):
         start_a1(0)
     with jax.named_scope("chunk1b"):
-        second_phase(1, 4, 8)
+        second_phase(1, 2, 4)
     with jax.named_scope("comm1b"):
         start_pair(1)
         start_a2(0)
     with jax.named_scope("chunk2a"):
-        second_phase(2, 0, 4)
+        second_phase(2, 0, 2)
     with jax.named_scope("comm2a"):
         start_a1(1)
-        start_b1(0)
+        start_b(0)
     with jax.named_scope("chunk2b"):
-        second_phase(2, 4, 8)
+        second_phase(2, 2, 4)
     with jax.named_scope("comm2b"):
         start_pair(2)
         start_a2(1)
-        start_b2(0)
+        finish(0)
     with jax.named_scope("tail_a1"):
         start_a1(2)
-        start_b1(1)
-        finish(0)
+        start_b(1)
     with jax.named_scope("tail_a2"):
         start_a2(2)
-        start_b2(1)
-    with jax.named_scope("tail_b1"):
-        start_b1(2)
         finish(1)
-    with jax.named_scope("tail_b2"):
-        start_b2(2)
+    with jax.named_scope("tail_b"):
+        start_b(2)
     with jax.named_scope("tail_end"):
         finish(2)
 
@@ -318,17 +334,23 @@
     with jax.named_scope("zstage"):
         def col(k):
             return dev(pool, ((zc + k) % 8) * 2 + core)
-        relay = send(zs.at[(zc + 4) % 8], zrel.at[0], sz.at[0], rz.at[0], col(7))
-        zcp = [send(zs.at[(zc + k) % 8], zr.at[k - 1], sz.at[k], rz.at[k], col(k)) for k in (3, 6, 2, 7, 1)]
-        relay.wait_recv()
-        zrel[1] = zs[(zc + 5) % 8] + zrel[0]
-        zcp.append(send(zrel.at[1], zr.at[4], sz.at[5], rz.at[5], col(5)))
+        zcp = [(k, send(zs.at[(zc + k) % 8], zr.at[k - 1], sz.at[k], rz.at[k], col(k))) for k in (4, 3, 5, 2, 6, 1, 7)]
+        for cp in grids:
+            cp.wait()
+        odd = pool % 2
+        wide = lax.broadcasted_iota(jnp.int32, (6, 128), 1)
+        for k in range(2):
+            v = flat[k, :, pl.ds(pl.multiple_of(576 * pool - 64 * odd, 128), 1408)]
+            v = jnp.where(odd == 1, pltpu.roll(v, 1408 - 64, 1), v)
+            wins = [v[:, 176 + 96 * w:304 + 96 * w] for w in range(-1, 11)]
+            for w in range(10):
+                gl[k, pl.ds(w, 6, stride=16), :] = jnp.where(wide < 16, wins[w + 2], jnp.where(wide >= 112, wins[w], wins[w + 1]))
+        gs = [send(gl.at[0, pl.ds(80, 16)], gr.at[0], sg.at[0], rg.at[0], dev(pool, (slab + 1) % 16)),
+              send(gl.at[0, pl.ds(0, 16)], gr.at[1], sg.at[1], rg.at[1], dev(pool, (slab + 15) % 16))]
         f = zs[zc]
-        for cp, k in zip(reversed(zcp[:-1]), (1, 7, 2, 6, 3)):
+        for k, cp in reversed(zcp):
             cp.wait_recv()
             f = f + zr[k - 1]
-        zcp[-1].wait_recv()
-        f = f + zr[4]
 
     with jax.named_scope("rows_out"):
         for c2 in range(2):
@@ -367,6 +389,7 @@
 
         def down(v, ax):
             return pltpu.roll(v, 1, ax)
+        g = [gl[0, pl.ds(16 * n, 16), :] for n in range(6)]
         flux = []
         for n in range(8):
             coef = gr[0] if n == 0 else gr[1] if n == 7 else g[n - 1]
@@ -377,13 +400,20 @@
             for ax in (0, 1):
                 slope = coef * ((up(rho, ax) - down(rho, ax)) * 0.5)
                 div = div + (up(slope, ax) - down(slope, ax)) * 0.5
-            out[n] = b[10 + n] + l[n] * rho - div
-
-    for cp in [*log.values(), *gs, relay, *zcp, *acp, *bcp]:
+            pot[pl.ds(16 * n, 16), :] = b[10 + n] + gl[1, pl.ds(16 * n, 16), :] * rho - div
+        row640 = lax.broadcasted_iota(jnp.int32, (6, 640), 1)
+        whole = jnp.zeros((6, 640), f32)
+        for w in range(6):
+            piece = jnp.concatenate([pot[pl.ds(w + 2, 6, stride=16), :], jnp.zeros((6, 512), f32)], axis=1)
+            piece = pltpu.roll(piece, (96 * w - 16) % 640, 1)
+            whole = jnp.where((row640 >= 96 * w) & (row640 < 96 * w + 96), piece, whole)
+        out[...] = whole[:, :576]
+
+    for cp in [*log.values(), *gs, *(cp for _, cp in zcp), *acp, *bcp]:
         cp.wait_send()
 
 
-def run(wave, resp, occ, idx, g, l):
+def run(wave, resp, occ, idx, grad, local):
     t, hu = np_tables()
     f32, bf = jnp.float32, jnp.bfloat16
     consts = [jnp.asarray(v, bf) for v in (t, *y_tables(t), dense_tables(hu), np.concatenate([hu, hu], axis=1))]
@@ -394,35 +424,26 @@
     buf = lambda *dims: pltpu.VMEM(dims, f32)
     return pl.pallas_call(
         kernel,
-        out_shape=jax.ShapeDtypeStruct((6, 16, 128), f32),
-        in_specs=[sm, sm, hbm, hbm, vm, vm] + [vm] * len(consts),
+        out_shape=jax.ShapeDtypeStruct((6, 576), f32),
+        in_specs=[sm, sm, hbm, hbm, hbm, hbm] + [hbm] * len(consts),
         out_specs=vm,
         scratch_shapes=[
+            *(pltpu.VMEM(v.shape, v.dtype) for v in consts),
             pltpu.VMEM((NB, 2, 96, BL), bf), pltpu.VMEM((NB, 2, 96, BL), bf),
-            buf(2, 9216, 128), buf(2, 9216, 128), buf(9, 768, 128), buf(9, 384, 128), buf(9, 4, 4, 3, 8, 128),
+            buf(2, 96 * STEP, 128), buf(2, 96 * STEP, 128), buf(9, 864, 128), buf(9, 432, 128), buf(9, 4, 4, 3, 8, 128),
             buf(9, 2, 4, 3, 8, 128), buf(9, 2, 4, 3, 8, 128), buf(9, 4, 3, 8, 128), buf(9, 4, 3, 8, 128),
-            buf(9, 2, 3, 8, 128), buf(9, 2, 3, 8, 128), buf(9, 3, 8, 128), buf(96, 384),
-            buf(8, 6, 16, 128), buf(2, 6, 16, 128), buf(7, 6, 16, 128), buf(256, 128), buf(256, 128),
-            buf(16, 16, 128), buf(16, 16, 128), buf(2, 16, 128),
-            dma((2, NB)), dma((9,)), dma((9,)), dma((9, 2)), dma((9, 2)), dma((9,)), dma((9,)), dma((9, 2)), dma((9, 2)),
-            dma((9,)), dma((9,)), dma((8,)), dma((8,)), dma((31,)), dma((31,)), dma((15,)), dma((15,)), dma((2,)), dma((2,)),
+            buf(9, 3, 3, 8, 128), buf(96, 384), buf(8, 6, 16, 128), buf(7, 6, 16, 128), buf(256, 128), buf(256, 128),
+            buf(16, 16, 128), buf(16, 16, 128), buf(2, 16, 128), buf(2, 6, 9984), buf(2, 96, 128), buf(96, 128),
+            dma((2, NB)), dma((12,)), dma((2, 3)), dma((9,)), dma((9,)), dma((9, 2)), dma((9, 2)), dma((9,)), dma((9,)), dma((9, 3)), dma((9, 3)),
+            dma((8,)), dma((8,)), dma((31,)), dma((31,)), dma((15,)), dma((15,)), dma((2,)), dma((2,)),
         ],
         compiler_params=pltpu.CompilerParams(collective_id=0, has_side_effects=True, vmem_limit_bytes=60 * 1024 * 1024),
         name="response",
-    )(occ, idx, wave, resp, g, l, *consts)
-
-
-def rows_of(flat, first):
-    grid = flat.reshape(6, N, N)
-    wide = jnp.concatenate([grid[:, 94:], grid, grid[:, :10]], axis=1)
-    part = lax.dynamic_slice_in_dim(wide, first, 16, 1)
-    return jnp.concatenate([part[..., 80:], part, part[..., :16]], axis=2)
+    )(occ, idx, wave, resp, grad, local, *consts)
 
 
 def shards(wave_coeff, response_coeff, band_index, occupation, local_kernel, gradient_kernel):
-    row = 6 * lax.axis_index("pool")
-    res = run(wave_coeff, response_coeff, occupation, band_index, rows_of(gradient_kernel, row), rows_of(local_kernel, row))
-    return res[:, 2:8, 16:112].reshape(6, 576)
+    return run(wave_coeff, response_coeff, occupation, band_index, gradient_kernel, local_kernel)
 
 
 def solution(mesh):

time: 86.1 us -> 70.8 us (0.82)
  Pallas kernels: 79.5 us -> 68.6 us
  local copies, waits for them, and re-layouts: 3.85 us -> 1.34 us
  other arithmetic: 1.5 us -> 0 us
    pallas_call x1, Pallas kernels: 79.5 us -> 68.6 us  [run(): pl.pallas_call(kernel, out_shape=jax.ShapeDtypeStruct((6, 576), f32), in_...]
    reshape x3 -> x0, local copies, waits for them, and re-layouts: 2.86 us -> none  [the longest x2 2.18 us: rows_of(): grid = flat.reshape(6, N, N)]
    concatenate x3 -> x0, other arithmetic: 1.5 us -> none  [the longest x2 1.43 us: rows_of(): return jnp.concatenate([part[..., 80:], part, part[..., :16]], axis=2)]
    unnamed x0 -> x1, local copies, waits for them, and re-layouts: none -> 1.34 us
    slice x7 -> x0, local copies, waits for them, and re-layouts: 0.99 us -> none  [the longest x1 0.81 us: shards(): return res[:, 2:8, 16:112].reshape(6, 576)]
where the time goes in v3:
time: 70.8 us; the launch traced here: 70.6 us
  Pallas kernels  68.6 us (97%)
  local copies, waits for them, and re-layouts  1.34 us (2%)
    pallas_call x1, Pallas kernels, run(): pl.pallas_call(kernel, out_shape=jax.ShapeDtypeStruct((6, 576), f32), in_...  68.6 us

profile of v3, /device:TPU:1, one launch (start us, length us, event | category | flops | bytes accessed | tf_op | source)
XLA Modules:
  0.0 70.6 jit_solution(6240278501408295318)
XLA Ops:
  0.7 68.6 %response.1 = f32[6,576]{1,0:T(8,128)} custom-call(s32[256]{0:T(256)} %occ.1, s32[1]{0:T(128)S(6)} %copy.20.idx, bf16[1,2,96,9216]{3,2,1,0:T(8,128)(2,1)} %wave.1, bf16[1,2,96,9216]{3,2,1,0:T(8,128)(2,1)} %resp.1, f32[6,9216]{1,0:T(8,128)} %grad.1, f32[6,9216]{1,0:T(8,128)} %local.1, bf16[192,192]{1,0:T(8,128)(2,1)} %constant.24.clone.refs_0_, ...), custom_call_target="tpu_custom_call" | custom-call | tf_op jit(solution)/shard_map/response/pallas_call | solution.py:425
  69.3 1.3 %copy.21 = f32[6,576]{1,0:T(8,128)} copy(f32[6,576]{1,0:T(8,128)} %response.1) | data formatting | bytes 27648

commit v4 on v3

v4 whole, which is shorter than its diff:
```python
import math

import numpy as np
import jax
import jax.numpy as jnp
from jax import lax
from jax.experimental import pallas as pl
from jax.experimental.pallas import tpu as pltpu
from jax.sharding import PartitionSpec as P

MESH = pl.DeviceIdType.MESH
full_turn = 2.0 * math.pi
N = 96
BL = 1536
NB = 9216 // BL
STEP = 97


def np_tables():
    k = np.arange(N)
    ang = (np.outer(k, k) % N) * (2 * np.pi / N)
    c, s = np.cos(ang) / np.sqrt(N), np.sin(ang) / np.sqrt(N)
    t = np.block([[c, -s], [s, c]])
    return t, np.cos(ang) + np.sin(ang)


def y_tables(t):
    outs = []
    for row in range(4):
        js = sorted({(96 * row) // 128, (96 * row + 95) // 128})
        w = np.zeros((256 * len(js), 256))
        for n, j in enumerate(js):
            for l in range(128):
                d = 128 * j + l
                if d // 96 != row:
                    continue
                for s in range(2):
                    for r in range(2):
                        w[256 * n + 128 * s + l, 128 * r:128 * r + 96] = t[96 * r:96 * r + 96, 96 * s + d % 96]
        outs.append(w)
    return outs


def dense_tables(hu):
    outs = []
    for j in range(3):
        w = np.zeros((256, 128))
        for l in range(128):
            q, ky = divmod(128 * j + l, 96)
            w[(q - j) * 128:(q - j) * 128 + 96, l] = hu[ky]
        outs.append(np.concatenate([w, w], axis=0))
    return np.stack(outs)


def inverse_tables(hu):
    hye = np.zeros((128, 128))
    hye[:N] = hu[:, (np.arange(128) - 16) % N] / N
    return [hu / math.sqrt(N), hye]


def x_table(hu):
    w = np.zeros((16, 16, 32, 8))
    for p in range(16):
        for i in range(10):
            w[p, i, :, :3] = (hu[(6 * p - 2 + i) % N] / N).reshape(32, 3)
    w = w.reshape(256, 256)
    hi = w.astype(jnp.bfloat16).astype(np.float64)
    return np.concatenate([hi, hi, w - hi], axis=1)


def exact(a, b):
    return jnp.dot(a, b, precision=lax.Precision.HIGHEST, preferred_element_type=jnp.float32)


def halves(v):
    hi = v.astype(jnp.bfloat16)
    return hi, (v - hi.astype(jnp.float32)).astype(jnp.bfloat16)


def swap(t):
    return t + 1 - 2 * (t % 2)


def mirror(t):
    return 3 - t


def kernel(occupation, numbers, wave, resp, grad, local, *refs):
    tables, out, held, refs = refs[:7], refs[7], refs[8:15], refs[15:]
    (occ, idx, cc, bw, br, d, pbuf, s, f1, t2, f3, zbuf, rbuf, zp, zpr, zv, zvr, q, a, xo, b, gr, flat, gl, pot,
     csem, tsem, gsem, osem, p_snd, p_rcv, s1, r1, s3, r3, sp, rp, sv, rv, sa, ra, sb, rb, sg, rg) = refs
    t_ref, wy, yd, hx, hz, hye, hxe = held
    f32, bf = jnp.float32, jnp.bfloat16
    pool, slab = lax.axis_index("pool"), lax.axis_index("slab")
    y, x = pool // 4, pool % 4
    zc, core = slab // 2, slab % 2
    other = 1 - core

    def load(k, blk):
        return pltpu.make_async_copy((wave, resp)[k].at[0, :, :, pl.ds(blk * BL, BL)], cc.at[blk, k], csem.at[blk])

    early = [pltpu.make_async_copy(tables[n], held[n], tsem.at[n]) for n in range(2)]
    late = [pltpu.make_async_copy(tables[n], held[n], tsem.at[n]) for n in range(2, 7)]
    for cp in early:
        cp.start()
    for blk in range(NB):
        for k in range(2):
            load(k, blk).start()
    for cp in late:
        cp.start()
    weights = [pltpu.make_async_copy(occupation, occ, osem.at[0]), pltpu.make_async_copy(numbers, idx, osem.at[1])]
    for cp in weights:
        cp.start()
    for k, src in enumerate((grad, local)):
        for lo, to, size in ((0, 384, 9216), (9216 - 384, 0, 384), (0, 9600, 384)):
            pltpu.make_async_copy(src.at[:, pl.ds(lo, size)], flat.at[k, :, pl.ds(to, size)], gsem.at[0]).start()

    def drain(ref, sem):
        pltpu.make_async_copy(ref, ref, sem).wait()


    def dev(p, sl):
        return {"pool": p, "slab": sl}

    def plane(k):
        dc, dp = k // 16, k % 16
        c2 = (core + dc) % 2
        p2 = (pool + dp) % 16
        return c2, p2, dev(p2, zc * 2 + c2)

    barrier = pltpu.get_barrier_semaphore()

    def hail(who):
        pl.semaphore_signal(barrier, inc=1, device_id=who, device_id_type=MESH)

    for k in range(1, 32):
        hail(plane(k)[2])
    for dz in range(1, 8):
        hail(dev(pool, (slab + 2 * dz) % 16))
    hail(dev(pool, (slab + 15 + 2 * core) % 16))
    for r in range(12, 16):
        hail(dev(r, (slab + (1 if r < 14 else 15)) % 16))

    def send(src, dst, ssem, rsem, who):
        cp = pltpu.make_async_remote_copy(src_ref=src, dst_ref=dst, send_sem=ssem, recv_sem=rsem, device_id=who, device_id_type=MESH)
        cp.start()
        return cp

    for ref in (q, a, b):
        ref[...] = jnp.zeros_like(ref)
    for cp in early:
        cp.wait()

    def first_phase(blk, carry):
        drain(cc.at[blk], csem.at[blk])
        t = t_ref[...]
        for k, dst in enumerate((bw, br)):
            c = jnp.concatenate([cc[blk, k, 0], cc[blk, k, 1]], axis=0)
            zb = jnp.dot(t, c, preferred_element_type=f32).astype(bf)
            groups = BL // 384
            for row, (lo, hi) in enumerate(((0, 256), (256, 768), (768, 1280), (1280, 1536))):
                js = sorted({(96 * row) // 128, (96 * row + 95) // 128})
                lhs = jnp.concatenate([
                    jnp.concatenate([zb[96 * r:96 * r + 96, 384 * n + 128 * j:384 * n + 128 * j + 128] for j in js for r in range(2)], axis=1)
                    for n in range(groups)], axis=0)
                res = jnp.dot(lhs, wy[lo:hi], preferred_element_type=f32)
                for n in range(groups):
                    base = (blk * (BL // 96) + 4 * n + row) * STEP
                    for r in range(2):
                        dst[r, pl.ds(base, 96), :] = res[96 * n:96 * n + 96, 128 * r:128 * r + 128]
        return carry

    def second_phase(chunk, first, last):
        def body(step, carry):
            t = t_ref[...]
            weight = occ[idx[0]].astype(f32) * (1.0 / 256.0)
            his, los = [], []
            for n in range(2):
                i = 2 * step + n
                spaces = []
                for src in (bw, br):
                    parts = []
                    for k in range(4):
                        z = chunk * 32 + 8 * k + i
                        parts.append(jnp.concatenate([src[r, pl.ds(z, 96, stride=STEP), :].astype(bf) for r in range(2)], axis=0))
                    spaces.append(jnp.dot(t, jnp.concatenate(parts, axis=1), preferred_element_type=f32))
                v, w = spaces
                hi, lo = halves((v[:96] * w[:96] + v[96:] * w[96:]) * weight)
                his.append(hi)
                los.append(lo)
            hi, lo = jnp.concatenate(his, axis=0), jnp.concatenate(los, axis=0)
            cols = []
            for j in range(3):
                lhs = jnp.concatenate([hi[:, 128 * j:128 * j + 256], lo[:, 128 * j:128 * j + 256]], axis=1)
                cols.append(jnp.dot(lhs, yd[j], preferred_element_type=f32))
            cols = jnp.concatenate([col[96 * n:96 * n + 96] for n in range(2) for col in cols], axis=1)
            gx = jnp.dot(hx[...], jnp.concatenate(halves(cols), axis=0), preferred_element_type=f32)
            for n in range(2):
                for j in range(3):
                    d[3 * chunk + j, pl.ds(2 * step + n, 96, stride=9), :] = gx[:, 384 * n + 128 * j:384 * n + 128 * j + 128]
            return carry
        lax.fori_loop(first, last, body, 0)


    def order(u, m, along):
        ax = (3 * u + m + along) % 2
        return (x, y)[ax], ax

    def at(ax, pos):
        return dev(y * 4 + pos, slab) if ax == 0 else dev(pos * 4 + x, slab)

    def units(c):
        return range(3 * c, 3 * c + 3)

    def start_pair(c):
        for u in units(c):
            send(d.at[u, pl.ds(pl.multiple_of(other * 432, 432), 432)], pbuf.at[u], p_snd.at[0], p_rcv.at[c], dev(pool, zc * 2 + other))

    def start_a(c):
        drain(pbuf.at[pl.ds(3 * c, 3)], p_rcv.at[c])
        for u in units(c):
            for n in range(48):
                s[u, n // 12, n // 3 % 4, n % 3] = d[u, pl.ds(core * 432 + 9 * n, 8), :] + pbuf[u, pl.ds(9 * n, 8), :]
            for m in range(3):
                pos, ax = order(u, m, 0)
                for k in (2, 1, 3):
                    to = (pos + k) % 4
                    src = s.at[u, :, to, m] if ax == 0 else s.at[u, to, :, m]
                    send(src, f1.at[u, m, k - 1], s1.at[0], r1.at[c], at(ax, to))

    def start_b(c):
        drain(f1.at[pl.ds(3 * c, 3)], r1.at[c])
        for u in units(c):
            for m in range(3):
                pos, ax = order(u, m, 0)
                part = s[u, :, pos, m] if ax == 0 else s[u, pos, :, m]
                for k in (1, 3, 2):
                    part = part + f1[u, m, k - 1]
                t2[u, m] = part
                pos, ax = order(u, m, 1)
                for k in (2, 1, 3):
                    to = (pos + k) % 4
                    send(t2.at[u, m, to], f3.at[u, m, k - 1], s3.at[0], r3.at[c], at(ax, to))

    lane = lax.broadcasted_iota(jnp.int32, (8, 128), 1)

    def finish(c):
        parts = {}
        drain(f3.at[pl.ds(3 * c, 3)], r3.at[c])
        for u in units(c):
            for m in range(3):
                part = t2[u, m, order(u, m, 1)[0]]
                for k in (1, 3, 2):
                    part = part + f3[u, m, k - 1]
                parts[u - 3 * c, m] = part
        for m in range(3):
            v = jnp.concatenate([parts[j, m] for j in range(3)], axis=1)
            for k in range(4):
                w = v if k == 0 else pltpu.roll(v, 384 - 96 * k, 1)
                zbuf[32 * c + 8 * k:32 * c + 8 * k + 8, 128 * m:128 * m + 128] = jnp.where(lane < 96, w[:, :128], 0.0)
        rows = jnp.concatenate([zbuf[32 * c:32 * c + 32, 128 * m:128 * m + 128] for m in range(3)], axis=0)
        both = exact(rows, hye[...])
        for m in range(3):
            rbuf[m, 32 * c:32 * c + 32, :] = both[32 * m:32 * m + 32]
        for zd in ((0, 1), (2, 3, 4), (5, 6, 7))[c]:
            for m in range(3):
                zp[zd, 12 * m:12 * m + 12, :] = rbuf[m, 12 * zd:12 * zd + 12, :]
            slot = (zd - zc + 15) % 8
            cp = pltpu.make_async_remote_copy(src_ref=zp.at[zd], dst_ref=zpr.at[slot], send_sem=sp.at[0], recv_sem=rp.at[0], device_id=dev(pool, 2 * zd + core), device_id_type=MESH)
            pl.when(zc != zd)(cp.start)

    with jax.named_scope("first_phase"):
        lax.fori_loop(0, NB, first_phase, 0)
    with jax.named_scope("chunk0"):
        for cp in late + weights:
            cp.wait()
        second_phase(0, 0, 4)
    with jax.named_scope("barrier"):
        pl.semaphore_wait(barrier, 39 + 16 * (pool // 12))
    start_pair(0)
    with jax.named_scope("chunk1a"):
        second_phase(1, 0, 2)
    with jax.named_scope("comm1a"):
        start_a(0)
    with jax.named_scope("chunk1b"):
        second_phase(1, 2, 4)
    start_pair(1)
    with jax.named_scope("chunk2a"):
        second_phase(2, 0, 2)
    with jax.named_scope("comm2a"):
        start_a(1)
    with jax.named_scope("chunk2b"):
        second_phase(2, 2, 4)
    start_pair(2)
    with jax.named_scope("tail_a2"):
        start_a(2)
    with jax.named_scope("tail_b0"):
        start_b(0)
    with jax.named_scope("tail_b1"):
        start_b(1)
    with jax.named_scope("tail_fin0"):
        finish(0)
    with jax.named_scope("tail_b2"):
        start_b(2)
    with jax.named_scope("tail_fin1"):
        finish(1)
    with jax.named_scope("tail_fin2"):
        finish(2)

    with jax.named_scope("solve"):
        zk = zbuf[...]
        vh = exact(hz[...], zk)
        kz = lax.broadcasted_iota(jnp.int32, (96, 128), 0)
        ky = lax.broadcasted_iota(jnp.int32, (96, 128), 1)
        qz = jnp.where(2 * kz >= N, kz - N, kz)
        qy = jnp.where(2 * ky >= N, ky - N, ky)
        zy = qz * qz + qy * qy
        scaled = []
        for m in range(3):
            kx = jnp.full((96, 128), 1, jnp.int32) * (3 * (core * 16 + pool) + m)
            qx = jnp.where(2 * kx >= N, kx - N, kx)
            squared = (zy + qx * qx).astype(f32) * ((full_turn / N) ** 2)
            screen = jnp.where(squared > 0, full_turn / jnp.where(squared > 0, squared, 1.0), 0.0)
            scaled.append(vh[:, 128 * m:128 * m + 128] * screen)
        vz = exact(hz[...], jnp.concatenate(scaled, axis=1))
        both = exact(jnp.concatenate([vz[:, 128 * m:128 * m + 128] for m in range(3)], axis=0), hye[...])
        for m in range(3):
            for zd in range(8):
                zv[zd, 12 * m:12 * m + 12, :] = both[96 * m + 12 * zd:96 * m + 12 * zd + 12]

    with jax.named_scope("zstage"):
        def col(k):
            return dev(pool, ((zc + k) % 8) * 2 + core)
        for k in (4, 3, 5, 2, 6, 1, 7):
            send(zv.at[(zc + k) % 8], zvr.at[k - 1], sv.at[0], rv.at[0], col(k))
        drain(flat, gsem.at[0])
        odd = pool % 2
        wide = lax.broadcasted_iota(jnp.int32, (6, 128), 1)
        for k in range(2):
            v = flat[k, :, pl.ds(pl.multiple_of(576 * pool - 64 * odd, 128), 1408)]
            v = jnp.where(odd == 1, pltpu.roll(v, 1408 - 64, 1), v)
            wins = [v[:, 176 + 96 * w:304 + 96 * w] for w in range(-1, 11)]
            for w in range(10):
                gl[k, pl.ds(w, 6, stride=16), :] = jnp.where(wide < 16, wins[w + 2], jnp.where(wide >= 112, wins[w], wins[w + 1]))
        send(gl.at[0, pl.ds(80, 16)], gr.at[0], sg.at[0], rg.at[0], dev(pool, (slab + 1) % 16))
        send(gl.at[0, pl.ds(0, 16)], gr.at[1], sg.at[0], rg.at[0], dev(pool, (slab + 15) % 16))

    me = core * 16 + pool
    mine = pl.ds(pl.multiple_of(me * 8, 8), 3)

    def deal(rows):
        for dc in range(2):
            c2 = (core + dc) % 2
            for r in rows:
                src = q.at[pl.ds(pl.multiple_of((c2 * 16 + r) * 8, 8), 3)]
                cp = pltpu.make_async_remote_copy(src_ref=src, dst_ref=a.at[mine], send_sem=sa.at[0], recv_sem=ra.at[0], device_id=dev(r, zc * 2 + c2), device_id_type=MESH)
                if dc:
                    cp.start()
                else:
                    pl.when(pool != r)(cp.start)

    with jax.named_scope("rows_rho"):
        drain(zpr, rp.at[0])
        f = zp[zc]
        for k in range(7):
            f = f + zpr[k]
        for c2 in range(2):
            for m in range(3):
                base = c2 * 128 + m
                rho6 = f[12 * m + 6 * c2:12 * m + 6 * c2 + 6]
                q[pl.ds(base, 6, stride=8), :] = rho6
                q[pl.ds(base + 96, 2, stride=8), :] = rho6[:2]
                q[pl.ds(base + 112, 2, stride=8), :] = rho6[4:]
        deal((0, 1, 2, 3, 4, 5, 12, 13, 14, 15))
    with jax.named_scope("rows_v"):
        drain(zvr, rv.at[0])
        f = zv[zc]
        for k in range(7):
            f = f + zvr[k]
        for c2 in range(2):
            for m in range(3):
                q[pl.ds(c2 * 128 + m + 48, 6, stride=8), :] = f[12 * m + 6 * c2:12 * m + 6 * c2 + 6]
        deal(range(6, 12))
    with jax.named_scope("rows_out"):
        a[mine, :] = q[pl.ds(pl.multiple_of((core * 16 + pool) * 8, 8), 3), :]
        drain(a.at[pl.ds(0, 93)], ra.at[0])
    with jax.named_scope("rows_back"):
        hi, lo = halves(a[...])
        xo[...] = jnp.dot(hxe[...], jnp.concatenate([hi, lo, hi], axis=0), preferred_element_type=f32).reshape(16, 16, 128)
        edge = pool // 12
        aim = (slab + 16 + edge * (2 * (pool // 14) - 1)) % 16
        for k in range(1, 16):
            p2 = (pool + k) % 16
            send(xo.at[p2, pl.ds(0, 10)], b.at[pool, pl.ds(0, 10)], sb.at[0], rb.at[0], dev(p2, aim))

        def across():
            return pltpu.make_async_remote_copy(src_ref=xo.at[pool, pl.ds(0, 10)], dst_ref=b.at[pool, pl.ds(0, 10)], send_sem=sb.at[1], recv_sem=rb.at[1], device_id=dev(pool, aim), device_id_type=MESH)

        @pl.when(edge == 0)
        def _():
            b[pool] = xo[pool]

        @pl.when(edge == 1)
        def _():
            across().start()
            across().wait()
        drain(gr, rg.at[0])
        drain(a.at[pl.ds(0, 150)], rb.at[0])

    with jax.named_scope("final"):
        def up(v, ax):
            return pltpu.roll(v, v.shape[ax] - 1, ax)

        def down(v, ax):
            return pltpu.roll(v, 1, ax)
        g = [gl[0, pl.ds(16 * n, 16), :] for n in range(6)]
        rhos = [b[n] for n in (14, 15, 0, 1, 2, 3, 4, 5, 12, 13)]
        flux = []
        for n in range(8):
            coef = gr[0] if n == 0 else gr[1] if n == 7 else g[n - 1]
            flux.append(coef * ((rhos[n + 2] - rhos[n]) * 0.5))
        for n in range(6):
            rho, coef = rhos[n + 2], g[n]
            div = (flux[n + 2] - flux[n]) * 0.5
            for ax in (0, 1):
                slope = coef * ((up(rho, ax) - down(rho, ax)) * 0.5)
                div = div + (up(slope, ax) - down(slope, ax)) * 0.5
            pot[pl.ds(16 * n, 16), :] = b[6 + n] + gl[1, pl.ds(16 * n, 16), :] * rho - div
        row640 = lax.broadcasted_iota(jnp.int32, (6, 640), 1)
        whole = jnp.zeros((6, 640), f32)
        for w in range(6):
            piece = jnp.concatenate([pot[pl.ds(w + 2, 6, stride=16), :], jnp.zeros((6, 512), f32)], axis=1)
            piece = pltpu.roll(piece, (96 * w - 16) % 640, 1)
            whole = jnp.where((row640 >= 96 * w) & (row640 < 96 * w + 96), piece, whole)
        out[...] = whole[:, :576]

    with jax.named_scope("sent"):
        for ref, sem in ((pbuf, p_snd), (f1, s1), (f3, s3), (zpr, sp), (zvr, sv), (gr, sg), (a.at[pl.ds(0, 93)], sa), (a.at[pl.ds(0, 150)], sb)):
            drain(ref, sem.at[0])


def run(wave, resp, occ, idx, grad, local):
    t, hu = np_tables()
    f32, bf = jnp.float32, jnp.bfloat16
    consts = [jnp.asarray(v, bf) for v in (t, np.concatenate(y_tables(t)), dense_tables(hu), np.concatenate([hu, hu], axis=1))]
    consts += [jnp.asarray(v, f32) for v in inverse_tables(hu)]
    consts.append(jnp.asarray(x_table(hu), bf))
    vm, hbm = pl.BlockSpec(memory_space=pltpu.VMEM), pl.BlockSpec(memory_space=pl.ANY)
    dma = pltpu.SemaphoreType.DMA
    buf = lambda *dims: pltpu.VMEM(dims, f32)
    return pl.pallas_call(
        kernel,
        out_shape=jax.ShapeDtypeStruct((6, 576), f32),
        in_specs=[hbm] * (6 + len(consts)),
        out_specs=vm,
        scratch_shapes=[
            *(pltpu.VMEM(v.shape, v.dtype) for v in consts),
            pltpu.SMEM((256,), jnp.int32), pltpu.SMEM((1,), jnp.int32),
            pltpu.VMEM((NB, 2, 2, 96, BL), bf),
            buf(2, 96 * STEP, 128), buf(2, 96 * STEP, 128), buf(9, 864, 128), buf(9, 432, 128), buf(9, 4, 4, 3, 8, 128),
            buf(9, 3, 3, 4, 8, 128), buf(9, 3, 4, 8, 128), buf(9, 3, 3, 8, 128), buf(96, 384), buf(3, 96, 128),
            buf(8, 36, 128), buf(7, 36, 128), buf(8, 36, 128), buf(7, 36, 128), buf(256, 128), buf(256, 128),
            buf(16, 16, 128), buf(16, 16, 128), buf(2, 16, 128), buf(2, 6, 9984), buf(2, 96, 128), buf(96, 128),
            dma((NB,)), dma((7,)), dma((1,)), dma((2,)), dma((1,)), dma((3,)), dma((1,)), dma((3,)), dma((1,)), dma((3,)),
            *(dma((1,)) for _ in range(6)), dma((2,)), dma((2,)), dma((1,)), dma((1,)),
        ],
        compiler_params=pltpu.CompilerParams(collective_id=0, has_side_effects=True, vmem_limit_bytes=60 * 1024 * 1024),
        name="response",
    )(occ, idx, wave, resp, grad, local, *consts)


def shards(wave_coeff, response_coeff, band_index, occupation, local_kernel, gradient_kernel):
    return run(wave_coeff, response_coeff, occupation, band_index, gradient_kernel, local_kernel)


def solution(mesh):
    return jax.shard_map(
        shards,
        mesh=mesh,
        in_specs=(
            P(("pool", "slab"), None, None, None),
            P(("pool", "slab"), None, None, None),
            P(("pool", "slab")),
            P(),
            P("slab", None),
            P("slab", None),
        ),
        out_specs=P("slab", "pool"),
        check_vma=False,
    )
```

time: 70.8 us -> 60.6 us (0.86)
  Pallas kernels: 68.6 us -> 58.5 us
    pallas_call x1, Pallas kernels: 68.6 us -> 58.5 us  [run(): pl.pallas_call(kernel, out_shape=jax.ShapeDtypeStruct((6, 576), f32), in_...]
where the time goes in v4:
time: 60.6 us; the launch traced here: 60.5 us
  Pallas kernels  58.5 us (97%)
  local copies, waits for them, and re-layouts  1.34 us (2%)
  between operations  0.66 us (1%)
    pallas_call x1, Pallas kernels, run(): pl.pallas_call(kernel, out_shape=jax.ShapeDtypeStruct((6, 576), f32), in_...  58.5 us
    unnamed x1, local copies, waits for them, and re-layouts  1.34 us

profile of v4, /device:TPU:1, one launch (start us, length us, event | category | flops | bytes accessed | tf_op | source)
XLA Modules:
  0.0 60.5 jit_solution(11612483552631958447)
XLA Ops:
  0.7 58.5 %response.1 = f32[6,576]{1,0:T(8,128)} custom-call(s32[256]{0:T(256)} %occupation.1, s32[1]{0:T(128)S(6)} %copy.15.numbers, bf16[1,2,96,9216]{3,2,1,0:T(8,128)(2,1)} %wave.1, bf16[1,2,96,9216]{3,2,1,0:T(8,128)(2,1)} %resp.1, f32[6,9216]{1,0:T(8,128)} %grad.1, f32[6,9216]{1,0:T(8,128)} %local.1, bf16[192,192]{1,0:T(8,128)(2,1)} %constant.14.clone.refs_0_, ...), custom_call_target="tpu_custom_call" | custom-call | tf_op jit(solution)/shard_map/response/pallas_call | solution.py:451
  59.2 1.3 %copy.16 = f32[6,576]{1,0:T(8,128)} copy(f32[6,576]{1,0:T(8,128)} %response.1) | data formatting | bytes 27648

commit v5 on v4

--- a/solution.py
+++ b/solution.py
@@ -26,17 +26,11 @@
 
 def y_tables(t):
     outs = []
-    for row in range(4):
-        js = sorted({(96 * row) // 128, (96 * row + 95) // 128})
-        w = np.zeros((256 * len(js), 256))
-        for n, j in enumerate(js):
-            for l in range(128):
-                d = 128 * j + l
-                if d // 96 != row:
-                    continue
-                for s in range(2):
-                    for r in range(2):
-                        w[256 * n + 128 * s + l, 128 * r:128 * r + 96] = t[96 * r:96 * r + 96, 96 * s + d % 96]
+    for skip in (0, 32):
+        w = np.zeros((256, 256))
+        for s in range(2):
+            for r in range(2):
+                w[128 * s + skip:128 * s + skip + 96, 128 * r:128 * r + 96] = t[96 * r:96 * r + 96, 96 * s:96 * s + 96].T
         outs.append(w)
     return outs
 
@@ -68,26 +62,19 @@
     return np.concatenate([hi, hi, w - hi], axis=1)
 
 
-def exact(a, b):
-    return jnp.dot(a, b, precision=lax.Precision.HIGHEST, preferred_element_type=jnp.float32)
-
-
 def halves(v):
     hi = v.astype(jnp.bfloat16)
     return hi, (v - hi.astype(jnp.float32)).astype(jnp.bfloat16)
 
 
-def swap(t):
-    return t + 1 - 2 * (t % 2)
-
-
-def mirror(t):
-    return 3 - t
+def close(a, b):
+    (ah, al), (bh, bl) = halves(a), halves(b)
+    return jnp.dot(jnp.concatenate([ah, ah, al], axis=1), jnp.concatenate([bh, bl, bh], axis=0), preferred_element_type=jnp.float32)
 
 
 def kernel(occupation, numbers, wave, resp, grad, local, *refs):
     tables, out, held, refs = refs[:7], refs[7], refs[8:15], refs[15:]
-    (occ, idx, cc, bw, br, d, pbuf, s, f1, t2, f3, zbuf, rbuf, zp, zpr, zv, zvr, q, a, xo, b, gr, flat, gl, pot,
+    (occ, idx, cc, rs, bw, br, d, pbuf, s, f1, t2, f3, zbuf, rbuf, zp, zpr, zv, zvr, q, a, xo, b, gr, flat, gl, pot,
      csem, tsem, gsem, osem, p_snd, p_rcv, s1, r1, s3, r3, sp, rp, sv, rv, sa, ra, sb, rb, sg, rg) = refs
     t_ref, wy, yd, hx, hz, hye, hxe = held
     f32, bf = jnp.float32, jnp.bfloat16
@@ -158,48 +145,50 @@
             c = jnp.concatenate([cc[blk, k, 0], cc[blk, k, 1]], axis=0)
             zb = jnp.dot(t, c, preferred_element_type=f32).astype(bf)
             groups = BL // 384
-            for row, (lo, hi) in enumerate(((0, 256), (256, 768), (768, 1280), (1280, 1536))):
-                js = sorted({(96 * row) // 128, (96 * row + 95) // 128})
+            for row, (start, lo) in enumerate(((0, 0), (96, 0), (192, 0), (256, 256))):
                 lhs = jnp.concatenate([
-                    jnp.concatenate([zb[96 * r:96 * r + 96, 384 * n + 128 * j:384 * n + 128 * j + 128] for j in js for r in range(2)], axis=1)
+                    jnp.concatenate([zb[96 * r:96 * r + 96, 384 * n + start:384 * n + start + 128] for r in range(2)], axis=1)
                     for n in range(groups)], axis=0)
-                res = jnp.dot(lhs, wy[lo:hi], preferred_element_type=f32)
+                res = jnp.dot(lhs, wy[lo:lo + 256], preferred_element_type=f32)
                 for n in range(groups):
                     base = (blk * (BL // 96) + 4 * n + row) * STEP
                     for r in range(2):
                         dst[r, pl.ds(base, 96), :] = res[96 * n:96 * n + 96, 128 * r:128 * r + 128]
         return carry
 
-    def second_phase(chunk, first, last):
-        def body(step, carry):
-            t = t_ref[...]
-            weight = occ[idx[0]].astype(f32) * (1.0 / 256.0)
-            his, los = [], []
-            for n in range(2):
-                i = 2 * step + n
-                spaces = []
-                for src in (bw, br):
-                    parts = []
-                    for k in range(4):
-                        z = chunk * 32 + 8 * k + i
-                        parts.append(jnp.concatenate([src[r, pl.ds(z, 96, stride=STEP), :].astype(bf) for r in range(2)], axis=0))
-                    spaces.append(jnp.dot(t, jnp.concatenate(parts, axis=1), preferred_element_type=f32))
-                v, w = spaces
-                hi, lo = halves((v[:96] * w[:96] + v[96:] * w[96:]) * weight)
-                his.append(hi)
-                los.append(lo)
-            hi, lo = jnp.concatenate(his, axis=0), jnp.concatenate(los, axis=0)
-            cols = []
-            for j in range(3):
-                lhs = jnp.concatenate([hi[:, 128 * j:128 * j + 256], lo[:, 128 * j:128 * j + 256]], axis=1)
-                cols.append(jnp.dot(lhs, yd[j], preferred_element_type=f32))
-            cols = jnp.concatenate([col[96 * n:96 * n + 96] for n in range(2) for col in cols], axis=1)
-            gx = jnp.dot(hx[...], jnp.concatenate(halves(cols), axis=0), preferred_element_type=f32)
-            for n in range(2):
-                for j in range(3):
-                    d[3 * chunk + j, pl.ds(2 * step + n, 96, stride=9), :] = gx[:, 384 * n + 128 * j:384 * n + 128 * j + 128]
-            return carry
-        lax.fori_loop(first, last, body, 0)
+    def to_space(chunk, planes):
+        t = t_ref[...]
+        weight = occ[idx[0]].astype(f32) * (1.0 / 256.0)
+        for lo in (0, 4):
+            spaces = []
+            for src in (bw, br):
+                parts = []
+                for k, i in planes[lo:lo + 4]:
+                    parts.append(jnp.concatenate([src[r, pl.ds(32 * chunk + 8 * k + i, 96, stride=STEP), :].astype(bf) for r in range(2)], axis=0))
+                spaces.append(jnp.dot(t, jnp.concatenate(parts, axis=1), preferred_element_type=f32))
+            v, w = spaces
+            pair = halves((v[:96] * w[:96] + v[96:] * w[96:]) * weight)
+            for n, (k, i) in enumerate(planes[lo:lo + 4]):
+                for h in range(2):
+                    rs[h, k, pl.ds(i * 96, 96), :] = pair[h][:, 128 * n:128 * n + 128]
+
+    def to_waves(u, j):
+        lhs = jnp.concatenate([rs[h, j + n] for h in range(2) for n in range(2)], axis=1)
+        col = jnp.dot(lhs, yd[j], preferred_element_type=f32)
+        col = jnp.concatenate([col[96 * i:96 * i + 96] for i in range(8)], axis=1)
+        gx = jnp.dot(hx[...], jnp.concatenate(halves(col), axis=0), preferred_element_type=f32)
+        for i in range(8):
+            d[u, pl.ds(i, 96, stride=9), :] = gx[:, 128 * i:128 * i + 128]
+
+    def unit(u):
+        c, j = divmod(u, 3)
+        with jax.named_scope(f"unit{u}"):
+            if j == 0:
+                to_space(c, [(k, i) for i in range(4) for k in range(2)])
+                to_space(c, [(k, i) for i in range(4, 8) for k in range(2)])
+            else:
+                to_space(c, [(j + 1, i) for i in range(8)])
+            to_waves(u, j)
 
 
     def order(u, m, along):
@@ -212,13 +201,12 @@
     def units(c):
         return range(3 * c, 3 * c + 3)
 
-    def start_pair(c):
-        for u in units(c):
-            send(d.at[u, pl.ds(pl.multiple_of(other * 432, 432), 432)], pbuf.at[u], p_snd.at[0], p_rcv.at[c], dev(pool, zc * 2 + other))
-
-    def start_a(c):
-        drain(pbuf.at[pl.ds(3 * c, 3)], p_rcv.at[c])
-        for u in units(c):
+    def start_pair(u):
+        send(d.at[u, pl.ds(pl.multiple_of(other * 432, 432), 432)], pbuf.at[u], p_snd.at[0], p_rcv.at[u], dev(pool, zc * 2 + other))
+
+    def start_a(u):
+        with jax.named_scope(f"a{u}"):
+            drain(pbuf.at[u], p_rcv.at[u])
             for n in range(48):
                 s[u, n // 12, n // 3 % 4, n % 3] = d[u, pl.ds(core * 432 + 9 * n, 8), :] + pbuf[u, pl.ds(9 * n, 8), :]
             for m in range(3):
@@ -226,11 +214,11 @@
                 for k in (2, 1, 3):
                     to = (pos + k) % 4
                     src = s.at[u, :, to, m] if ax == 0 else s.at[u, to, :, m]
-                    send(src, f1.at[u, m, k - 1], s1.at[0], r1.at[c], at(ax, to))
-
-    def start_b(c):
-        drain(f1.at[pl.ds(3 * c, 3)], r1.at[c])
-        for u in units(c):
+                    send(src, f1.at[u, m, k - 1], s1.at[0], r1.at[u], at(ax, to))
+
+    def start_b(u):
+        with jax.named_scope(f"b{u}"):
+            drain(f1.at[u], r1.at[u])
             for m in range(3):
                 pos, ax = order(u, m, 0)
                 part = s[u, :, pos, m] if ax == 0 else s[u, pos, :, m]
@@ -240,7 +228,7 @@
                 pos, ax = order(u, m, 1)
                 for k in (2, 1, 3):
                     to = (pos + k) % 4
-                    send(t2.at[u, m, to], f3.at[u, m, k - 1], s3.at[0], r3.at[c], at(ax, to))
+                    send(t2.at[u, m, to], f3.at[u, m, k - 1], s3.at[0], r3.at[u // 3], at(ax, to))
 
     lane = lax.broadcasted_iota(jnp.int32, (8, 128), 1)
 
@@ -259,7 +247,7 @@
                 w = v if k == 0 else pltpu.roll(v, 384 - 96 * k, 1)
                 zbuf[32 * c + 8 * k:32 * c + 8 * k + 8, 128 * m:128 * m + 128] = jnp.where(lane < 96, w[:, :128], 0.0)
         rows = jnp.concatenate([zbuf[32 * c:32 * c + 32, 128 * m:128 * m + 128] for m in range(3)], axis=0)
-        both = exact(rows, hye[...])
+        both = close(rows, hye[...])
         for m in range(3):
             rbuf[m, 32 * c:32 * c + 32, :] = both[32 * m:32 * m + 32]
         for zd in ((0, 1), (2, 3, 4), (5, 6, 7))[c]:
@@ -271,45 +259,32 @@
 
     with jax.named_scope("first_phase"):
         lax.fori_loop(0, NB, first_phase, 0)
-    with jax.named_scope("chunk0"):
-        for cp in late + weights:
-            cp.wait()
-        second_phase(0, 0, 4)
+    for cp in late + weights:
+        cp.wait()
+    unit(0)
     with jax.named_scope("barrier"):
         pl.semaphore_wait(barrier, 39 + 16 * (pool // 12))
     start_pair(0)
-    with jax.named_scope("chunk1a"):
-        second_phase(1, 0, 2)
-    with jax.named_scope("comm1a"):
-        start_a(0)
-    with jax.named_scope("chunk1b"):
-        second_phase(1, 2, 4)
-    start_pair(1)
-    with jax.named_scope("chunk2a"):
-        second_phase(2, 0, 2)
-    with jax.named_scope("comm2a"):
-        start_a(1)
-    with jax.named_scope("chunk2b"):
-        second_phase(2, 2, 4)
-    start_pair(2)
-    with jax.named_scope("tail_a2"):
-        start_a(2)
-    with jax.named_scope("tail_b0"):
-        start_b(0)
-    with jax.named_scope("tail_b1"):
-        start_b(1)
-    with jax.named_scope("tail_fin0"):
+    for u in range(1, 9):
+        unit(u)
+        start_pair(u)
+        start_a(u - 1)
+        if u >= 5:
+            start_b(u - 5)
+    start_a(8)
+    start_b(4)
+    with jax.named_scope("finish0"):
         finish(0)
-    with jax.named_scope("tail_b2"):
-        start_b(2)
-    with jax.named_scope("tail_fin1"):
+    for u in (5, 6, 7, 8):
+        start_b(u)
+    with jax.named_scope("finish1"):
         finish(1)
-    with jax.named_scope("tail_fin2"):
+    with jax.named_scope("finish2"):
         finish(2)
 
     with jax.named_scope("solve"):
         zk = zbuf[...]
-        vh = exact(hz[...], zk)
+        vh = close(hz[...], zk)
         kz = lax.broadcasted_iota(jnp.int32, (96, 128), 0)
         ky = lax.broadcasted_iota(jnp.int32, (96, 128), 1)
         qz = jnp.where(2 * kz >= N, kz - N, kz)
@@ -322,8 +297,8 @@
             squared = (zy + qx * qx).astype(f32) * ((full_turn / N) ** 2)
             screen = jnp.where(squared > 0, full_turn / jnp.where(squared > 0, squared, 1.0), 0.0)
             scaled.append(vh[:, 128 * m:128 * m + 128] * screen)
-        vz = exact(hz[...], jnp.concatenate(scaled, axis=1))
-        both = exact(jnp.concatenate([vz[:, 128 * m:128 * m + 128] for m in range(3)], axis=0), hye[...])
+        vz = close(hz[...], jnp.concatenate(scaled, axis=1))
+        both = close(jnp.concatenate([vz[:, 128 * m:128 * m + 128] for m in range(3)], axis=0), hye[...])
         for m in range(3):
             for zd in range(8):
                 zv[zd, 12 * m:12 * m + 12, :] = both[96 * m + 12 * zd:96 * m + 12 * zd + 12]
@@ -445,23 +420,23 @@
     consts = [jnp.asarray(v, bf) for v in (t, np.concatenate(y_tables(t)), dense_tables(hu), np.concatenate([hu, hu], axis=1))]
     consts += [jnp.asarray(v, f32) for v in inverse_tables(hu)]
     consts.append(jnp.asarray(x_table(hu), bf))
-    vm, hbm = pl.BlockSpec(memory_space=pltpu.VMEM), pl.BlockSpec(memory_space=pl.ANY)
+    vm, hbm = pl.BlockSpec(memory_space=pltpu.VMEM), pl.BlockSpec(memory_space=pltpu.HBM)
     dma = pltpu.SemaphoreType.DMA
     buf = lambda *dims: pltpu.VMEM(dims, f32)
     return pl.pallas_call(
         kernel,
-        out_shape=jax.ShapeDtypeStruct((6, 576), f32),
+        out_shape=pltpu.VMEM((6, 576), f32),
         in_specs=[hbm] * (6 + len(consts)),
         out_specs=vm,
         scratch_shapes=[
             *(pltpu.VMEM(v.shape, v.dtype) for v in consts),
             pltpu.SMEM((256,), jnp.int32), pltpu.SMEM((1,), jnp.int32),
-            pltpu.VMEM((NB, 2, 2, 96, BL), bf),
+            pltpu.VMEM((NB, 2, 2, 96, BL), bf), pltpu.VMEM((2, 4, 768, 128), bf),
             buf(2, 96 * STEP, 128), buf(2, 96 * STEP, 128), buf(9, 864, 128), buf(9, 432, 128), buf(9, 4, 4, 3, 8, 128),
             buf(9, 3, 3, 4, 8, 128), buf(9, 3, 4, 8, 128), buf(9, 3, 3, 8, 128), buf(96, 384), buf(3, 96, 128),
             buf(8, 36, 128), buf(7, 36, 128), buf(8, 36, 128), buf(7, 36, 128), buf(256, 128), buf(256, 128),
             buf(16, 16, 128), buf(16, 16, 128), buf(2, 16, 128), buf(2, 6, 9984), buf(2, 96, 128), buf(96, 128),
-            dma((NB,)), dma((7,)), dma((1,)), dma((2,)), dma((1,)), dma((3,)), dma((1,)), dma((3,)), dma((1,)), dma((3,)),
+            dma((NB,)), dma((7,)), dma((1,)), dma((2,)), dma((1,)), dma((9,)), dma((1,)), dma((9,)), dma((1,)), dma((3,)),
             *(dma((1,)) for _ in range(6)), dma((2,)), dma((2,)), dma((1,)), dma((1,)),
         ],
         compiler_params=pltpu.CompilerParams(collective_id=0, has_side_effects=True, vmem_limit_bytes=60 * 1024 * 1024),

time: 60.6 us -> 55.6 us (0.917)
  Pallas kernels: 58.5 us -> 54.3 us
  local copies, waits for them, and re-layouts: 1.34 us -> 0.61 us
    pallas_call x1, Pallas kernels: 58.5 us -> 54.3 us  [run(): pl.pallas_call(kernel, out_shape=pltpu.VMEM((6, 576), f32), in_specs=[hbm...]
    unnamed x1, local copies, waits for them, and re-layouts: 1.34 us -> 0.61 us
where the time goes in v5:
time: 55.6 us; the launch traced here: 55.5 us
  Pallas kernels  54.3 us (98%)
  between operations  0.66 us (1%)
  local copies, waits for them, and re-layouts  0.61 us (1%)
    pallas_call x1, Pallas kernels, run(): pl.pallas_call(kernel, out_shape=pltpu.VMEM((6, 576), f32), in_specs=[hbm...  54.3 us

profile of v5, /device:TPU:1, one launch (start us, length us, event | category | flops | bytes accessed | tf_op | source)
XLA Modules:
  0.0 55.5 jit_solution(17152258406753510460)
XLA Ops:
  0.7 54.3 %response.1 = f32[6,576]{1,0:T(8,128)S(1)} custom-call(s32[256]{0:T(256)} %occupation.1, s32[1]{0:T(128)S(6)} %copy.16.numbers, bf16[1,2,96,9216]{3,2,1,0:T(8,128)(2,1)} %wave.1, bf16[1,2,96,9216]{3,2,1,0:T(8,128)(2,1)} %resp.1, f32[6,9216]{1,0:T(8,128)} %grad.1, f32[6,9216]{1,0:T(8,128)} %local.1, bf16[192,192]{1,0:T(8,128)(2,1)} %constant.14.clone.refs_0_, ...), custom_call_target="tpu_custom_call" | custom-call | tf_op jit(solution)/shard_map/response/pallas_call | solution.py:426
  54.9 0.6 %copy.15 = f32[6,576]{1,0:T(8,128)} copy(f32[6,576]{1,0:T(8,128)S(1)} %response.1) | data formatting | bytes 27648

commit v6 on v5

--- a/solution.py
+++ b/solution.py
@@ -42,7 +42,7 @@
         for l in range(128):
             q, ky = divmod(128 * j + l, 96)
             w[(q - j) * 128:(q - j) * 128 + 96, l] = hu[ky]
-        outs.append(np.concatenate([w, w], axis=0))
+        outs.append(w)
     return np.stack(outs)
 
 
@@ -167,13 +167,12 @@
                     parts.append(jnp.concatenate([src[r, pl.ds(32 * chunk + 8 * k + i, 96, stride=STEP), :].astype(bf) for r in range(2)], axis=0))
                 spaces.append(jnp.dot(t, jnp.concatenate(parts, axis=1), preferred_element_type=f32))
             v, w = spaces
-            pair = halves((v[:96] * w[:96] + v[96:] * w[96:]) * weight)
+            rho = ((v[:96] * w[:96] + v[96:] * w[96:]) * weight).astype(bf)
             for n, (k, i) in enumerate(planes[lo:lo + 4]):
-                for h in range(2):
-                    rs[h, k, pl.ds(i * 96, 96), :] = pair[h][:, 128 * n:128 * n + 128]
+                rs[k, pl.ds(i * 96, 96), :] = rho[:, 128 * n:128 * n + 128]
 
     def to_waves(u, j):
-        lhs = jnp.concatenate([rs[h, j + n] for h in range(2) for n in range(2)], axis=1)
+        lhs = jnp.concatenate([rs[j], rs[j + 1]], axis=1)
         col = jnp.dot(lhs, yd[j], preferred_element_type=f32)
         col = jnp.concatenate([col[96 * i:96 * i + 96] for i in range(8)], axis=1)
         gx = jnp.dot(hx[...], jnp.concatenate(halves(col), axis=0), preferred_element_type=f32)
@@ -268,14 +267,18 @@
     for u in range(1, 9):
         unit(u)
         start_pair(u)
-        start_a(u - 1)
-        if u >= 5:
-            start_b(u - 5)
+        if u >= 2:
+            start_a(u - 2)
+        if u >= 7:
+            start_b(u - 7)
+    start_a(7)
+    start_b(2)
     start_a(8)
-    start_b(4)
+    for u in (3, 4, 5):
+        start_b(u)
     with jax.named_scope("finish0"):
         finish(0)
-    for u in (5, 6, 7, 8):
+    for u in (6, 7, 8):
         start_b(u)
     with jax.named_scope("finish1"):
         finish(1)
@@ -431,7 +434,7 @@
         scratch_shapes=[
             *(pltpu.VMEM(v.shape, v.dtype) for v in consts),
             pltpu.SMEM((256,), jnp.int32), pltpu.SMEM((1,), jnp.int32),
-            pltpu.VMEM((NB, 2, 2, 96, BL), bf), pltpu.VMEM((2, 4, 768, 128), bf),
+            pltpu.VMEM((NB, 2, 2, 96, BL), bf), pltpu.VMEM((4, 768, 128), bf),
             buf(2, 96 * STEP, 128), buf(2, 96 * STEP, 128), buf(9, 864, 128), buf(9, 432, 128), buf(9, 4, 4, 3, 8, 128),
             buf(9, 3, 3, 4, 8, 128), buf(9, 3, 4, 8, 128), buf(9, 3, 3, 8, 128), buf(96, 384), buf(3, 96, 128),
             buf(8, 36, 128), buf(7, 36, 128), buf(8, 36, 128), buf(7, 36, 128), buf(256, 128), buf(256, 128),

time: 55.6 us -> 54 us (0.971)
  Pallas kernels: 54.3 us -> 52.6 us
    pallas_call x1, Pallas kernels: 54.3 us -> 52.6 us  [run(): pl.pallas_call(kernel, out_shape=pltpu.VMEM((6, 576), f32), in_specs=[hbm...]
where the time goes in v6:
time: 54 us; the launch traced here: 53.9 us
  Pallas kernels  52.6 us (97%)
  between operations  0.66 us (1%)
  local copies, waits for them, and re-layouts  0.61 us (1%)
    pallas_call x1, Pallas kernels, run(): pl.pallas_call(kernel, out_shape=pltpu.VMEM((6, 576), f32), in_specs=[hbm...  52.6 us

profile of v6, /device:TPU:1, one launch (start us, length us, event | category | flops | bytes accessed | tf_op | source)
XLA Modules:
  0.0 53.9 jit_solution(12068122214300328740)
XLA Ops:
  0.7 52.6 %response.1 = f32[6,576]{1,0:T(8,128)S(1)} custom-call(s32[256]{0:T(256)} %occupation.1, s32[1]{0:T(128)S(6)} %copy.16.numbers, bf16[1,2,96,9216]{3,2,1,0:T(8,128)(2,1)} %wave.1, bf16[1,2,96,9216]{3,2,1,0:T(8,128)(2,1)} %resp.1, f32[6,9216]{1,0:T(8,128)} %grad.1, f32[6,9216]{1,0:T(8,128)} %local.1, bf16[192,192]{1,0:T(8,128)(2,1)} %constant.14.clone.refs_0_, ...), custom_call_target="tpu_custom_call" | custom-call | tf_op jit(solution)/shard_map/response/pallas_call | solution.py:429
  53.3 0.6 %copy.15 = f32[6,576]{1,0:T(8,128)} copy(f32[6,576]{1,0:T(8,128)S(1)} %response.1) | data formatting | bytes 27648

commit v7 on v6

--- a/solution.py
+++ b/solution.py
@@ -11,7 +11,7 @@
 MESH = pl.DeviceIdType.MESH
 full_turn = 2.0 * math.pi
 N = 96
-BL = 1536
+BL = 3072
 NB = 9216 // BL
 STEP = 97
 

time: 54 us -> 52.2 us (0.967)
  Pallas kernels: 52.6 us -> 50.8 us
    pallas_call x1, Pallas kernels: 52.6 us -> 50.8 us  [run(): pl.pallas_call(kernel, out_shape=pltpu.VMEM((6, 576), f32), in_specs=[hbm...]
where the time goes in v7:
time: 52.2 us; the launch traced here: 52.1 us
  Pallas kernels  50.8 us (97%)
  between operations  0.66 us (1%)
  local copies, waits for them, and re-layouts  0.61 us (1%)
    pallas_call x1, Pallas kernels, run(): pl.pallas_call(kernel, out_shape=pltpu.VMEM((6, 576), f32), in_specs=[hbm...  50.8 us

profile of v7, /device:TPU:1, one launch (start us, length us, event | category | flops | bytes accessed | tf_op | source)
XLA Modules:
  0.0 52.1 jit_solution(17602949828874033052)
XLA Ops:
  0.7 50.8 %response.1 = f32[6,576]{1,0:T(8,128)S(1)} custom-call(s32[256]{0:T(256)} %occupation.1, s32[1]{0:T(128)S(6)} %copy.16.numbers, bf16[1,2,96,9216]{3,2,1,0:T(8,128)(2,1)} %wave.1, bf16[1,2,96,9216]{3,2,1,0:T(8,128)(2,1)} %resp.1, f32[6,9216]{1,0:T(8,128)} %grad.1, f32[6,9216]{1,0:T(8,128)} %local.1, bf16[192,192]{1,0:T(8,128)(2,1)} %constant.14.clone.refs_0_, ...), custom_call_target="tpu_custom_call" | custom-call | tf_op jit(solution)/shard_map/response/pallas_call | solution.py:429
  51.5 0.6 %copy.15 = f32[6,576]{1,0:T(8,128)} copy(f32[6,576]{1,0:T(8,128)S(1)} %response.1) | data formatting | bytes 27648

commit v8 on v7

--- a/solution.py
+++ b/solution.py
@@ -274,12 +274,10 @@
     start_a(7)
     start_b(2)
     start_a(8)
-    for u in (3, 4, 5):
+    for u in range(3, 9):
         start_b(u)
     with jax.named_scope("finish0"):
         finish(0)
-    for u in (6, 7, 8):
-        start_b(u)
     with jax.named_scope("finish1"):
         finish(1)
     with jax.named_scope("finish2"):

time: 52.2 us -> 52.3 us (level)
  no operation moved by 1% of the time
where the time goes in v8:
time: 52.3 us; the launch traced here: 52.2 us
  Pallas kernels  51 us (98%)
  between operations  0.66 us (1%)
  local copies, waits for them, and re-layouts  0.61 us (1%)
    pallas_call x1, Pallas kernels, run(): pl.pallas_call(kernel, out_shape=pltpu.VMEM((6, 576), f32), in_specs=[hbm...  51 us

profile of v8, /device:TPU:1, one launch (start us, length us, event | category | flops | bytes accessed | tf_op | source)
XLA Modules:
  0.0 52.2 jit_solution(12457246595382107049)
XLA Ops:
  0.7 51.0 %response.1 = f32[6,576]{1,0:T(8,128)S(1)} custom-call(s32[256]{0:T(256)} %occupation.1, s32[1]{0:T(128)S(6)} %copy.16.numbers, bf16[1,2,96,9216]{3,2,1,0:T(8,128)(2,1)} %wave.1, bf16[1,2,96,9216]{3,2,1,0:T(8,128)(2,1)} %resp.1, f32[6,9216]{1,0:T(8,128)} %grad.1, f32[6,9216]{1,0:T(8,128)} %local.1, bf16[192,192]{1,0:T(8,128)(2,1)} %constant.14.clone.refs_0_, ...), custom_call_target="tpu_custom_call" | custom-call | tf_op jit(solution)/shard_map/response/pallas_call | solution.py:427
  51.6 0.6 %copy.15 = f32[6,576]{1,0:T(8,128)} copy(f32[6,576]{1,0:T(8,128)S(1)} %response.1) | data formatting | bytes 27648
